TPU v7x, 128 devices: a whole 4x4x4 slice. The times are simulated.
128 devices in a mesh: data: 1, sp: 128 (over z, y, x, core).
Axes of the slice: x: 4, y: 4, z: 4, core: 2. Of those that a mesh axis runs over, the one named last changes fastest.
Arguments:
- latents: bfloat16 [1, 256, 256, 384], P('data', 'sp')
- cotangent: bfloat16 [1, 256, 256, 384], P('data', 'sp')
- ln_params: bfloat16 [2, 4, 384], replicated
- w_qkv: bfloat16 [2, 384, 1152], replicated
- w_out: bfloat16 [2, 6, 64, 384], replicated
- w_up: bfloat16 [2, 384, 1536], replicated
- w_down: bfloat16 [2, 1536, 384], replicated
Outputs:
- output 1: bfloat16 [1, 256, 256, 384], P('data', 'sp')
- output 2: bfloat16 [1, 256, 256, 384], P('data', 'sp')
- output 3: float32 [2, 4, 384], P('data')
- output 4: float32 [2, 384, 1152], P('data')
- output 5: float32 [2, 6, 64, 384], P('data')
- output 6: float32 [2, 384, 1536], P('data')
- output 7: float32 [2, 1536, 384], P('data')
All inputs are finite; a program needn't handle non-finite values.
Results may differ from a plain program's by a relative error of at most 0.02.
Values are sent between devices in bfloat16 or wider.
A program may use at most 1 GiB of HBM per device.

v0:
```python
import jax
import jax.numpy as jnp
from jax import lax
from jax.sharding import PartitionSpec as P

SPATIAL = ('bamhe,banhe->bahmn', 'bahmn,banhe->bamhe', 'bahmn,bamhe->banhe')
TEMPORAL = ('bmche,bnche->bchmn', 'bchmn,bnche->bmche', 'bchmn,bmche->bnche')


def layer_norm(resid32, ln_gain, ln_shift):
    row_mean = jnp.mean(resid32, axis=-1, keepdims=True)
    centered = resid32 - row_mean
    inv_std = lax.rsqrt(jnp.mean(centered * centered, axis=-1, keepdims=True) + 1e-6)
    normed = centered * inv_std
    return (normed * ln_gain + ln_shift).astype(jnp.bfloat16), normed, inv_std


def layer_norm_back(d_ln_out, normed, inv_std, ln_gain):
    d_out32 = d_ln_out.astype(jnp.float32)
    d_gain = jnp.sum(d_out32 * normed, axis=(0, 1, 2))
    d_shift = jnp.sum(d_out32, axis=(0, 1, 2))
    d_norm = d_out32 * ln_gain
    d_center = d_norm - jnp.mean(d_norm, axis=-1, keepdims=True)
    d_resid = inv_std * (d_center - normed * jnp.mean(d_norm * normed, axis=-1, keepdims=True))
    return d_resid, d_gain, d_shift


def gelu_tanh(pre_act):
    return jax.nn.gelu(pre_act, approximate=True)


def qkv_forward(block_in32, ln_f32, w_qkv, num_heads):
    model_width = w_qkv.shape[0]
    a_in, normed, inv_std = layer_norm(block_in32, ln_f32[0], ln_f32[1])
    w_heads = w_qkv.reshape(model_width, 3, num_heads, model_width // num_heads)
    qkv_heads = jnp.einsum('bacd,dkhe->kbache', a_in, w_heads, preferred_element_type=jnp.float32)
    return qkv_heads.astype(jnp.bfloat16), (a_in, normed, inv_std)


def attend_forward(qkv_heads, attn_forms):
    score_scale = qkv_heads.shape[-1] ** -0.5
    scores = jnp.einsum(attn_forms[0], qkv_heads[0], qkv_heads[1], preferred_element_type=jnp.float32) * score_scale
    attn_probs = jax.nn.softmax(scores, axis=-1).astype(jnp.bfloat16)
    attn_out = jnp.einsum(attn_forms[1], attn_probs, qkv_heads[2], preferred_element_type=jnp.float32)
    return attn_out.astype(jnp.bfloat16), attn_probs


def tail_forward(block_in32, attn_out, ln_f32, w_out, w_up, w_down):
    attn_proj = jnp.einsum('bache,hef->bacf', attn_out, w_out, preferred_element_type=jnp.float32)
    hid32 = (block_in32 + attn_proj).astype(jnp.bfloat16).astype(jnp.float32)
    m_in, normed, inv_std = layer_norm(hid32, ln_f32[2], ln_f32[3])
    up_proj = jnp.dot(m_in, w_up, preferred_element_type=jnp.float32)
    act_out = gelu_tanh(up_proj).astype(jnp.bfloat16)
    block_out = (hid32 + jnp.dot(act_out, w_down, preferred_element_type=jnp.float32)).astype(jnp.bfloat16)
    return block_out, (m_in, normed, inv_std, up_proj, act_out)


def tail_backward(d_block_out, attn_out, tail_saved, ln_f32, w_out, w_up, w_down):
    m_in, normed, inv_std, up_proj, act_out = tail_saved
    g_down = jnp.einsum('bacf,bacd->fd', act_out, d_block_out, preferred_element_type=jnp.float32)
    d_act = jnp.einsum('bacd,fd->bacf', d_block_out, w_down, preferred_element_type=jnp.float32).astype(jnp.bfloat16)
    gelu_pull = jax.vjp(gelu_tanh, up_proj)[1]
    d_up = gelu_pull(d_act.astype(jnp.float32))[0].astype(jnp.bfloat16)
    g_up = jnp.einsum('bacd,bacf->df', m_in, d_up, preferred_element_type=jnp.float32)
    d_m_in = jnp.einsum('bacf,df->bacd', d_up, w_up, preferred_element_type=jnp.float32).astype(jnp.bfloat16)
    d_hid32, g_gain, g_shift = layer_norm_back(d_m_in, normed, inv_std, ln_f32[2])
    d_hid = (d_hid32 + d_block_out.astype(jnp.float32)).astype(jnp.bfloat16)
    g_out = jnp.einsum('bache,bacf->hef', attn_out, d_hid, preferred_element_type=jnp.float32)
    d_attn = jnp.einsum('bacf,hef->bache', d_hid, w_out, preferred_element_type=jnp.float32).astype(jnp.bfloat16)
    return d_attn, d_hid, (g_gain, g_shift, g_out, g_up, g_down)


def attend_backward(d_attn, qkv_heads, attn_probs, attn_forms):
    score_scale = qkv_heads.shape[-1] ** -0.5
    d_probs = jnp.einsum(attn_forms[0], d_attn, qkv_heads[2], preferred_element_type=jnp.float32)
    d_probs = d_probs.astype(jnp.bfloat16).astype(jnp.float32)
    probs32 = attn_probs.astype(jnp.float32)
    row_dot = jnp.sum(d_probs * probs32, axis=-1, keepdims=True)
    d_scores = (probs32 * (d_probs - row_dot) * score_scale).astype(jnp.bfloat16)
    d_query = jnp.einsum(attn_forms[1], d_scores, qkv_heads[1], preferred_element_type=jnp.float32).astype(jnp.bfloat16)
    d_key = jnp.einsum(attn_forms[2], d_scores, qkv_heads[0], preferred_element_type=jnp.float32).astype(jnp.bfloat16)
    d_value = jnp.einsum(attn_forms[2], attn_probs, d_attn, preferred_element_type=jnp.float32).astype(jnp.bfloat16)
    return jnp.stack([d_query, d_key, d_value])


def qkv_backward(d_qkv, d_hid, head_saved, ln_f32, w_qkv):
    a_in, normed, inv_std = head_saved
    model_width = w_qkv.shape[0]
    w_heads = w_qkv.reshape(model_width, 3, d_qkv.shape[-2], d_qkv.shape[-1])
    g_qkv = jnp.einsum('bacd,kbache->dkhe', a_in, d_qkv, preferred_element_type=jnp.float32)
    d_a_in = jnp.einsum('kbache,dkhe->bacd', d_qkv, w_heads, preferred_element_type=jnp.float32).astype(jnp.bfloat16)
    d_in32, g_gain, g_shift = layer_norm_back(d_a_in, normed, inv_std, ln_f32[0])
    d_block_in = (d_in32 + d_hid.astype(jnp.float32)).astype(jnp.bfloat16)
    return d_block_in, (g_gain, g_shift, g_qkv.reshape(model_width, 3 * model_width))


def block_forward(block_in, ln_params, w_qkv, w_out, w_up, w_down, attn_forms):
    ln_f32 = ln_params.astype(jnp.float32)
    block_in32 = block_in.astype(jnp.float32)
    qkv_heads, head_saved = qkv_forward(block_in32, ln_f32, w_qkv, w_out.shape[0])
    attn_out, attn_probs = attend_forward(qkv_heads, attn_forms)
    block_out, tail_saved = tail_forward(block_in32, attn_out, ln_f32, w_out, w_up, w_down)
    return block_out, (head_saved, qkv_heads, attn_probs, attn_out, tail_saved)


def block_backward(d_block_out, saved, ln_params, w_qkv, w_out, w_up, w_down, attn_forms):
    head_saved, qkv_heads, attn_probs, attn_out, tail_saved = saved
    ln_f32 = ln_params.astype(jnp.float32)
    d_attn, d_hid, tail_grads = tail_backward(d_block_out, attn_out, tail_saved, ln_f32, w_out, w_up, w_down)
    d_qkv = attend_backward(d_attn, qkv_heads, attn_probs, attn_forms)
    d_block_in, head_grads = qkv_backward(d_qkv, d_hid, head_saved, ln_f32, w_qkv)
    ln_grads = jnp.stack([head_grads[0], head_grads[1], tail_grads[0], tail_grads[1]])
    return d_block_in, (ln_grads, head_grads[2], tail_grads[2], tail_grads[3], tail_grads[4])


def device_step(latents, cotangent, ln_params, w_qkv, w_out, w_up, w_down):
    spatial_w = (ln_params[0], w_qkv[0], w_out[0], w_up[0], w_down[0])
    temporal_w = (ln_params[1], w_qkv[1], w_out[1], w_up[1], w_down[1])
    mid_act, spatial_saved = block_forward(latents, *spatial_w, SPATIAL)
    mid_swap = lax.all_to_all(mid_act, 'sp', 2, 1, tiled=True)
    out_swap, temporal_saved = block_forward(mid_swap, *temporal_w, TEMPORAL)
    result = lax.all_to_all(out_swap, 'sp', 1, 2, tiled=True)
    cot_swap = lax.all_to_all(cotangent, 'sp', 2, 1, tiled=True)
    d_mid_swap, temporal_grads = block_backward(cot_swap, temporal_saved, *temporal_w, TEMPORAL)
    d_mid = lax.all_to_all(d_mid_swap, 'sp', 1, 2, tiled=True)
    latents_grad, spatial_grads = block_backward(d_mid, spatial_saved, *spatial_w, SPATIAL)
    weight_grads = lax.psum([jnp.stack([grad_s, grad_t]) for grad_s, grad_t in zip(spatial_grads, temporal_grads)], 'sp')
    return (result, latents_grad) + tuple(weight_grads)


def solution(mesh):
    act_spec = P('data', 'sp', None, None)
    replicated = P()
    part_spec = P('data')
    return jax.shard_map(device_step, mesh=mesh,
                         in_specs=(act_spec, act_spec, replicated, replicated, replicated, replicated, replicated),
                         out_specs=(act_spec, act_spec, part_spec, part_spec, part_spec, part_spec, part_spec),
                         check_vma=False)
```

profile of v0, /device:TPU:1, one launch (start us, length us, event | category | flops | bytes accessed | tf_op | source)
XLA Modules:
  0.0 381.5 jit_solution(5021189335029658034)
XLA Ops:
  11.0 2.5 fusion.160
  16.0 2.5 fusion.161
  24.9 11.5 %all-to-all-start = ((bf16[1,2,256,384]{3,1,0,2:T(2,128)(2,1)}), bf16[1,2,256,384]{3,1,0,2:T(2,128)(2,1)S(1)}, u32[]{:S(2)}, u32[]{:S(2)}) async-start(bf16[1,2,256,384]{3,1,0,2:T(2,128)(2,1)} %copy.139), calls=%async_computation | async-start | bytes 786432 | tf_op jit(solution)/shard_map/all_to_all | solution.py:120
  37.6 2.2 copy.148
  41.2 7.2 %all-to-all-done = bf16[1,2,256,384]{3,1,0,2:T(2,128)(2,1)S(1)} async-done(((bf16[1,2,256,384]{3,1,0,2:T(2,128)(2,1)}), bf16[1,2,256,384]{3,1,0,2:T(2,128)(2,1)S(1)}, u32[]{:S(2)}, u32[]{:S(2)}) %all-to-all-start) | async-done | bytes 393248 | tf_op jit(solution)/shard_map/all_to_all | solution.py:120
  48.4 5.8 %all-to-all-start.2 = ((bf16[1,2,256,384]{3,1,0,2:T(2,128)(2,1)}), bf16[1,2,256,384]{3,1,0,2:T(2,128)(2,1)}, u32[]{:S(2)}, u32[]{:S(2)}) async-start(bf16[1,2,256,384]{3,1,0,2:T(2,128)(2,1)} %copy.154), calls=%async_computation.2 | async-start | bytes 786432 | tf_op jit(solution)/shard_map/all_to_all | solution.py:123
  61.0 2.4 multiply_reduce_fusion.7
  70.6 2.2 copy.140
  72.8 2.0 copy.224
  74.8 1.9 reshape.611
  78.4 2.0 fusion.47
  81.0 2.5 fusion.163
  87.4 3.0 fusion.10
  90.4 2.7 convolution_bitcast_fusion
  93.2 1.7 multiply_reduce_fusion.2
  97.0 1.8 convolution_convert_fusion.3
  98.8 4.9 %fusion.72 = bf16[1,1,256,2,6,64]{2,5,4,3,1,0:T(8,128)(2,1)} fusion(bf16[2,6,256,256]{2,3,1,0:T(8,128)(2,1)} %copy-done, bf16[2,6,256,256]{2,3,1,0:T(8,128)(2,1)} %convolution_convert_fusion.3, bf16[3,1,256,2,6,64]{2,5,4,0,3,1:T(8,128)(2,1)} %copy-done.6), kind=kOutput, calls=%fused_computation.121 | convolution fusion | flops 107941120 | bytes 7077888 | tf_op jit(solution)/shard_map/bchmn,bnche->bmche/dot_general | solution.py:80
  103.7 4.9 %fusion.71 = bf16[1,1,256,2,6,64]{2,5,4,3,1,0:T(8,128)(2,1)} fusion(bf16[2,6,256,256]{2,3,1,0:T(8,128)(2,1)} %copy-done, bf16[2,6,256,256]{2,3,1,0:T(8,128)(2,1)} %convolution_convert_fusion.3, bf16[3,1,256,2,6,64]{2,5,4,0,3,1:T(8,128)(2,1)} %copy-done.6), kind=kOutput, calls=%fused_computation.120 | convolution fusion | flops 107941120 | bytes 7077888 | tf_op jit(solution)/shard_map/bchmn,bmche->bnche/dot_general | solution.py:81
  113.9 2.4 multiply_reduce_fusion.3
  116.4 2.1 convolution_bitcast_fusion.4
  120.0 10.3 %all-to-all-start.3 = ((bf16[1,256,2,384]{3,2,0,1:T(2,128)(2,1)}), bf16[1,256,2,384]{3,2,0,1:T(2,128)(2,1)}, u32[]{:S(2)}, u32[]{:S(2)}) async-start(bf16[1,256,2,384]{3,2,0,1:T(2,128)(2,1)} %copy.160), calls=%async_computation.3 | async-start | bytes 786432 | tf_op jit(solution)/shard_map/all_to_all | solution.py:125
  130.5 2.3 convolution_bitcast_fusion.11
  132.8 3.7 convolution_bitcast_fusion.2
  136.6 5.4 %all-to-all-done.3 = bf16[1,256,2,384]{3,2,0,1:T(2,128)(2,1)} async-done(((bf16[1,256,2,384]{3,2,0,1:T(2,128)(2,1)}), bf16[1,256,2,384]{3,2,0,1:T(2,128)(2,1)}, u32[]{:S(2)}, u32[]{:S(2)}) %all-to-all-start.3) | async-done | bytes 393248 | tf_op jit(solution)/shard_map/all_to_all | solution.py:125
  142.0 2.4 copy_bitcast_fusion
  144.4 1.9 reshape.613
  146.3 5.0 %fusion.15 = bf16[2,256,1536]{2,1,0:T(8,128)(2,1)S(1)} fusion(f32[2,256,1536]{2,1,0:T(8,128)} %copy-done.15, bf16[2,256,384]{2,1,0:T(8,128)(2,1)} %reshape.613, bf16[2,1536,384]{2,1,0:T(8,128)(2,1)} %param.13), kind=kOutput, calls=%fused_computation.32 | convolution fusion | flops 621281280 | bytes 6291456 | tf_op jit(solution)/shard_map/bacd,fd->bacf/dot_general | solution.py:61
  151.4 2.7 convolution_bitcast_fusion.1
  154.1 2.5 fusion.111
  156.6 2.3 convolution_bitcast_fusion.3
  158.9 2.6 reshape.617
  162.3 1.9 fusion.159
  164.1 1.7 fusion.115
  168.1 2.8 convolution_convert_fusion.2
  170.9 3.2 fusion.74
  174.0 3.9 %fusion.73 = bf16[1,1,2,256,6,64]{3,5,4,2,1,0:T(8,128)(2,1)} fusion(bf16[2,6,256,256]{2,3,1,0:T(8,128)(2,1)S(1)} %divide_convert_fusion.1, bf16[2,6,256,256]{2,3,1,0:T(8,128)(2,1)} %convolution_convert_fusion.2, bf16[3,1,2,256,6,64]{3,5,4,0,2,1:T(8,128)(2,1)} %copy-done.25), kind=kOutput, calls=%fused_computation.122 | convolution fusion | flops 107941120 | bytes 7077888 | tf_op jit(solution)/shard_map/bahmn,bamhe->banhe/dot_general | solution.py:81
  181.5 2.7 pad_maximum_fusion.1
  185.6 2.5 pad_maximum_fusion
  190.0 2.2 pad_maximum_fusion.2
  192.3 3.4 fusion.75
  196.9 4.5 %all-to-all-start.1 = ((bf16[1,256,2,384]{3,2,0,1:T(2,128)(2,1)}), bf16[1,256,2,384]{3,2,0,1:T(2,128)(2,1)S(1)}, u32[]{:S(2)}, u32[]{:S(2)}) async-start(bf16[1,256,2,384]{3,2,0,1:T(2,128)(2,1)} %copy.151), calls=%async_computation.1 | async-start | bytes 786432 | tf_op jit(solution)/shard_map/all_to_all | solution.py:122
  201.6 14.0 %all-to-all-done.1 = bf16[1,256,2,384]{3,2,0,1:T(2,128)(2,1)S(1)} async-done(((bf16[1,256,2,384]{3,2,0,1:T(2,128)(2,1)}), bf16[1,256,2,384]{3,2,0,1:T(2,128)(2,1)S(1)}, u32[]{:S(2)}, u32[]{:S(2)}) %all-to-all-start.1) | async-done | bytes 393248 | tf_op jit(solution)/shard_map/all_to_all | solution.py:122
  216.8 2.2 fusion.109
  219.2 63.6 %psum.35 = f32[2,4,384]{2,1,0:T(4,128)} all-reduce(f32[2,4,384]{2,1,0:T(4,128)S(1)} %pad_maximum_fusion.8), channel_id=1, replica_groups=mesh['data'=1,'sp'=128] {'sp'}, use_global_device_ids=true, to_apply=%region_30.0 | all-reduce | flops 3072 | bytes 24576 | tf_op jit(solution)/shard_map/psum | solution.py:127
  283.9 79.7 %all-reduce.3.cloned.1.call-done = (f32[2,384,1152]{2,1,0:T(8,128)}, f32[2,6,64,384]{3,2,1,0:T(8,128)}, f32[2,384,1536]{2,1,0:T(8,128)}, f32[2,1536,384]{2,1,0:T(8,128)}) async-done(((f32[2,384,1152]{2,1,0:T(8,128)}, f32[2,6,64,384]{3,2,1,0:T(8,128)}, f32[2,384,1536]{2,1,0:T(8,128)}, f32[2,1536,384]{2,1,0:T(8,128)}), (f32[2,384,1152]{2,1,0:T(8,128)}, f32[2,6,64,384]{3,2,1,0:T(8,128)}, ...) | async-done | bytes 14155792 | tf_op jit(solution)/shard_map/psum | solution.py:127
  363.6 4.2 %copy.229 = f32[2,384,1152]{2,1,0:T(8,128)} copy(f32[2,384,1152]{2,1,0:T(8,128)} %get-tuple-element.58) | data formatting | bytes 7077888
  368.8 2.4 copy.231
  372.2 2.2 copy.232
  (226 shorter events, 60.0 us)
Async XLA Ops:
  7.2 7.2 %copy-start.7 = (bf16[1,2,256,384]{3,2,1,0:T(8,128)(2,1)S(1)}, bf16[1,2,256,384]{3,2,1,0:T(8,128)(2,1)}, u32[]{:S(2)}) copy-start(bf16[1,2,256,384]{3,2,1,0:T(8,128)(2,1)} %param.7) | copy-start | bytes 1179652
  8.4 7.0 %copy-start.50 = (f32[2,256]{1,0:T(2,128)}, f32[2,256]{1,0:T(2,128)S(1)}, u32[]{:S(2)}) copy-start(f32[2,256]{1,0:T(2,128)S(1)} %broadcast_multiply_fusion.11) | copy-start | bytes 6148
  9.7 5.7 %copy-start.55 = (f32[2,256]{1,0:T(2,128)}, f32[2,256]{1,0:T(2,128)S(1)}, u32[]{:S(2)}) copy-start(f32[2,256]{1,0:T(2,128)S(1)} %add_rsqrt_fusion.3) | copy-start | bytes 6148
  11.0 4.4 %copy-start.48 = (f32[384]{0:T(512)}, f32[384]{0:T(512)S(1)}, u32[]{:S(2)}) copy-start(f32[384]{0:T(512)S(1)} %get-tuple-element.30) | copy-start | bytes 4612
  11.0 4.4 %copy-start.57 = (f32[384]{0:T(512)}, f32[384]{0:T(512)S(1)}, u32[]{:S(2)}) copy-start(f32[384]{0:T(512)S(1)} %get-tuple-element.29) | copy-start | bytes 4612
  15.4 3.5 copy-start.25
  19.6 2.5 copy-start.27
  20.1 3.2 copy-start.41
  22.1 14.3 %copy-start.39 = (bf16[1,2,256,384]{3,2,1,0:T(8,128)(2,1)S(1)}, bf16[1,2,256,384]{3,2,1,0:T(8,128)(2,1)}, u32[]{:S(2)}) copy-start(bf16[1,2,256,384]{3,2,1,0:T(8,128)(2,1)} %param.8) | copy-start | bytes 1179652
  24.9 23.5 %all-to-all-start = ((bf16[1,2,256,384]{3,1,0,2:T(2,128)(2,1)}), bf16[1,2,256,384]{3,1,0,2:T(2,128)(2,1)S(1)}, u32[]{:S(2)}, u32[]{:S(2)}) async-start(bf16[1,2,256,384]{3,1,0,2:T(2,128)(2,1)} %copy.139), calls=%async_computation | async-start | bytes 786432 | tf_op jit(solution)/shard_map/all_to_all | solution.py:120
  48.4 5.8 %copy-start.14 = (bf16[1,2,256,384]{3,1,0,2:T(2,128)(2,1)}, bf16[1,2,256,384]{3,1,0,2:T(2,128)(2,1)S(1)}, u32[]{:S(2)}) copy-start(bf16[1,2,256,384]{3,1,0,2:T(2,128)(2,1)S(1)} %all-to-all-done) | copy-start | bytes 1179652
  48.4 24.4 %all-to-all-start.2 = ((bf16[1,2,256,384]{3,1,0,2:T(2,128)(2,1)}), bf16[1,2,256,384]{3,1,0,2:T(2,128)(2,1)}, u32[]{:S(2)}, u32[]{:S(2)}) async-start(bf16[1,2,256,384]{3,1,0,2:T(2,128)(2,1)} %copy.154), calls=%async_computation.2 | async-start | bytes 786432 | tf_op jit(solution)/shard_map/all_to_all | solution.py:123
  80.3 16.7 %copy-start.6 = (bf16[3,1,256,2,6,64]{2,5,4,0,3,1:T(8,128)(2,1)}, bf16[3,1,256,2,6,64]{2,5,4,0,3,1:T(8,128)(2,1)S(1)}, u32[]{:S(2)}) copy-start(bf16[3,1,256,2,6,64]{2,5,4,0,3,1:T(8,128)(2,1)S(1)} %fusion.47) | copy-start | bytes 3538948
  83.8 11.8 %copy-start = (bf16[2,6,256,256]{2,3,1,0:T(8,128)(2,1)}, bf16[2,6,256,256]{2,3,1,0:T(8,128)(2,1)S(1)}, u32[]{:S(2)}) copy-start(bf16[2,6,256,256]{2,3,1,0:T(8,128)(2,1)S(1)} %divide_convert_fusion) | copy-start | bytes 4718596
  83.8 2.5 copy-start.19
  84.2 3.2 copy-start.13
  85.4 9.5 %copy-start.43 = (f32[256,2]{0,1:T(2,128)}, f32[256,2]{0,1:T(2,128)S(1)}, u32[]{:S(2)}) copy-start(f32[256,2]{0,1:T(2,128)S(1)} %broadcast_multiply_fusion.4) | copy-start | bytes 6148
  85.7 9.2 %copy-start.46 = (f32[256,2]{0,1:T(2,128)}, f32[256,2]{0,1:T(2,128)S(1)}, u32[]{:S(2)}) copy-start(f32[256,2]{0,1:T(2,128)S(1)} %add_rsqrt_fusion) | copy-start | bytes 6148
  87.4 3.0 copy-start.17
  90.4 2.8 copy-start.29
  113.9 2.5 copy-start.52
  120.0 22.0 %all-to-all-start.3 = ((bf16[1,256,2,384]{3,2,0,1:T(2,128)(2,1)}), bf16[1,256,2,384]{3,2,0,1:T(2,128)(2,1)}, u32[]{:S(2)}, u32[]{:S(2)}) async-start(bf16[1,256,2,384]{3,2,0,1:T(2,128)(2,1)} %copy.160), calls=%async_computation.3 | async-start | bytes 786432 | tf_op jit(solution)/shard_map/all_to_all | solution.py:125
  130.3 233.2 %all-reduce.3.cloned.1.call-start = ((), (), s32[]{:S(2)}) async-start(), calls=%async_computation.4 | async-start | bytes 28311552 | tf_op jit(solution)/shard_map/psum | solution.py:127
  146.3 5.0 %copy-start.16 = (f32[2,256,1536]{2,1,0:T(8,128)S(1)}, f32[2,256,1536]{2,1,0:T(8,128)}, u32[]{:S(2)}) copy-start(f32[2,256,1536]{2,1,0:T(8,128)} %copy-done.15) | copy-start | bytes 9437188
  146.3 5.0 %copy-start.40 = (bf16[2,256,384]{2,1,0:T(8,128)(2,1)S(1)}, bf16[2,256,384]{2,1,0:T(8,128)(2,1)}, u32[]{:S(2)}) copy-start(bf16[2,256,384]{2,1,0:T(8,128)(2,1)} %reshape.613) | copy-start | bytes 1179652
  151.3 2.8 copy-start.20
  151.3 2.8 copy-start.42
  151.4 2.8 copy-start.45
  161.5 4.4 %copy-start.28 = (bf16[2,256,6,64]{1,3,2,0:T(8,128)(2,1)S(1)}, bf16[2,256,6,64]{1,3,2,0:T(8,128)(2,1)}, u32[]{:S(2)}) copy-start(bf16[2,256,6,64]{1,3,2,0:T(8,128)(2,1)} %copy-done.27) | copy-start | bytes 1179652
  161.5 5.6 %copy-start.33 = (bf16[2,6,64,384]{3,2,1,0:T(8,128)(2,1)S(1)}, bf16[2,6,64,384]{3,2,1,0:T(8,128)(2,1)}, u32[]{:S(2)}) copy-start(bf16[2,6,64,384]{3,2,1,0:T(8,128)(2,1)} %param.11) | copy-start | bytes 1769476
  181.5 2.7 copy-start.1
  181.5 4.1 %copy-start.2 = (f32[1,384,1536]{2,1,0:T(8,128)S(1)}, f32[1,384,1536]{2,1,0:T(8,128)}, u32[]{:S(2)}) copy-start(f32[1,384,1536]{2,1,0:T(8,128)} %convolution_bitcast_fusion.3) | copy-start | bytes 7077892
  185.6 2.5 copy-start.23
  185.6 2.5 copy-start.24
  192.3 9.2 %copy-start.61 = (f32[384]{0:T(512)S(1)}, f32[384]{0:T(512)}, u32[]{:S(2)}) copy-start(f32[384]{0:T(512)} %get-tuple-element.11) | copy-start | bytes 4612
  192.3 9.2 %copy-start.60 = (f32[384]{0:T(512)S(1)}, f32[384]{0:T(512)}, u32[]{:S(2)}) copy-start(f32[384]{0:T(512)} %get-tuple-element.22) | copy-start | bytes 4612
  192.3 9.2 %copy-start.63 = (f32[384]{0:T(512)S(1)}, f32[384]{0:T(512)}, u32[]{:S(2)}) copy-start(f32[384]{0:T(512)} %get-tuple-element.9) | copy-start | bytes 4612
  192.3 9.2 %copy-start.62 = (f32[384]{0:T(512)S(1)}, f32[384]{0:T(512)}, u32[]{:S(2)}) copy-start(f32[384]{0:T(512)} %get-tuple-element.21) | copy-start | bytes 4612
  195.7 21.0 %copy-start.64 = (f32[384]{0:T(512)S(1)}, f32[384]{0:T(512)}, u32[]{:S(2)}) copy-start(f32[384]{0:T(512)} %get-tuple-element.7) | copy-start | bytes 4612
  195.7 21.0 %copy-start.59 = (f32[384]{0:T(512)S(1)}, f32[384]{0:T(512)}, u32[]{:S(2)}) copy-start(f32[384]{0:T(512)} %get-tuple-element.19) | copy-start | bytes 4612
  195.7 21.0 %copy-start.36 = (bf16[1,1,2,256,6,64]{3,5,4,2,1,0:T(8,128)(2,1)S(1)}, bf16[1,1,2,256,6,64]{3,5,4,2,1,0:T(8,128)(2,1)}, u32[]{:S(2)}) copy-start(bf16[1,1,2,256,6,64]{3,5,4,2,1,0:T(8,128)(2,1)} %fusion.73) | copy-start | bytes 1179652
  196.9 18.6 %all-to-all-start.1 = ((bf16[1,256,2,384]{3,2,0,1:T(2,128)(2,1)}), bf16[1,256,2,384]{3,2,0,1:T(2,128)(2,1)S(1)}, u32[]{:S(2)}, u32[]{:S(2)}) async-start(bf16[1,256,2,384]{3,2,0,1:T(2,128)(2,1)} %copy.151), calls=%async_computation.1 | async-start | bytes 786432 | tf_op jit(solution)/shard_map/all_to_all | solution.py:122
  216.8 66.0 %copy-start.9 = (bf16[1,2,256,384]{3,2,1,0:T(8,128)(2,1)S(1)}, bf16[1,2,256,384]{3,2,1,0:T(8,128)(2,1)}, u32[]{:S(2)}) copy-start(bf16[1,2,256,384]{3,2,1,0:T(8,128)(2,1)} %copy-done.8) | copy-start | bytes 1179652
  363.6 5.2 %slice-start.2 = ((s8[4718592]{0:T(1024)(128)(4,1)}), s8[4194304]{0:T(1024)(128)(4,1)S(1)}, s32[]{:S(2)}) async-start(s8[4718592]{0:T(1024)(128)(4,1)} %bitcast.350), calls=%async_computation.7 | async-start | bytes 8388608
  363.6 4.2 %copy-start.34 = (f32[2,6,64,384]{3,2,1,0:T(8,128)S(1)}, f32[2,6,64,384]{3,2,1,0:T(8,128)}, u32[]{:S(2)}) copy-start(f32[2,6,64,384]{3,2,1,0:T(8,128)} %get-tuple-element.59) | copy-start | bytes 3538948
  363.6 5.2 %slice-start.3 = ((s8[4718592]{0:T(1024)(128)(4,1)}), s8[524288]{0:T(1024)(128)(4,1)S(1)}, s32[]{:S(2)}) async-start(s8[4718592]{0:T(1024)(128)(4,1)} %bitcast.350), calls=%async_computation.8 | async-start | bytes 1048576
  367.7 4.1 %slice-start = ((s8[4718592]{0:T(1024)(128)(4,1)}), s8[4194304]{0:T(1024)(128)(4,1)S(1)}, s32[]{:S(2)}) async-start(s8[4718592]{0:T(1024)(128)(4,1)} %bitcast.348), calls=%async_computation.5 | async-start | bytes 8388608
  368.8 3.4 slice-start.1
  (28 other events, 47.9 us)
Sparse Core Ops, SparseCore 0:
  192.4 171.1 all-reduce.2
where the time goes:
time: 389 us; the launch traced here: 381 us
  waiting for transfers between devices  106 us (27%)
  matrix products  72 us (19%)
  blocking collectives  63.6 us (16%)
  local copies, waits for them, and re-layouts  53.1 us (14%)
  other arithmetic  39 us (10%)
  starting transfers between devices  32.3 us (8%)
  between operations  15.3 us (4%)
    psum x1, waiting for transfers between devices, device_step(): lax.psum([jnp.stack([grad_s, grad_t]) for grad_s, grad_t in zip(spatial_g...  79.7 us
    psum x1, blocking collectives, device_step(): lax.psum([jnp.stack([grad_s, grad_t]) for grad_s, grad_t in zip(spatial_g...  63.6 us
    unnamed x147, local copies, waits for them, and re-layouts  18.4 us
    all_to_all x1, waiting for transfers between devices, device_step(): result = lax.all_to_all(out_swap, 'sp', 1, 2, tiled=True)  14 us
    all_to_all x1, starting transfers between devices, device_step(): mid_swap = lax.all_to_all(mid_act, 'sp', 2, 1, tiled=True)  11.5 us
    all_to_all x1, starting transfers between devices, device_step(): d_mid = lax.all_to_all(d_mid_swap, 'sp', 1, 2, tiled=True)  10.3 us
    dot_general x2, matrix products, attend_backward(): jnp.einsum(attn_forms[2], d_scores, qkv_heads[0], preferred_element_type=...  8.85 us
    another operation x7, other arithmetic, device_step(): jnp.stack([grad_s, grad_t])  8.58 us
  transfers between devices with their start and end apart: 5, of which 4 were waited for; matrix products, arithmetic and copies ran while one was open for 10% of the time, Pallas kernels for 0%

commit v1 on v0

v1 whole, which is shorter than its diff:
```python
import functools

import jax
import jax.numpy as jnp
from jax import lax
from jax.experimental import pallas as pl
from jax.experimental.pallas import tpu as pltpu
from jax.sharding import PartitionSpec as P

F32 = jnp.float32
BF16 = jnp.bfloat16
D = 384
T = 512
SEQ = 256
FF = 1536
ROWS = 128
MESH = pl.DeviceIdType.MESH
VMEM_LIMIT = 60 * 1024 * 1024
GELU_C = 0.7978845608028654
GELU_A = 0.044715


def dot_nn(a, b):
    return lax.dot_general(a, b, (((1,), (0,)), ((), ())), preferred_element_type=F32)


def dot_nt(a, b):
    return lax.dot_general(a, b, (((1,), (1,)), ((), ())), preferred_element_type=F32)


def dot_tn(a, b):
    return lax.dot_general(a, b, (((0,), (0,)), ((), ())), preferred_element_type=F32)


def row_tiles(body):
    def step(i, _):
        body(pl.ds(pl.multiple_of(i * ROWS, ROWS), ROWS))
        return 0
    lax.fori_loop(0, T // ROWS, step, 0)


def ln_norm(x32):
    mean = jnp.sum(x32, axis=-1, keepdims=True) * (1.0 / D)
    centered = x32 - mean
    inv_std = lax.rsqrt(jnp.sum(centered * centered, axis=-1, keepdims=True) * (1.0 / D) + 1e-6)
    return centered * inv_std, inv_std


def ln_back(d32, normed, inv_std, gain):
    d_norm = d32 * gain
    d_center = d_norm - jnp.sum(d_norm, axis=-1, keepdims=True) * (1.0 / D)
    return inv_std * (d_center - normed * (jnp.sum(d_norm * normed, axis=-1, keepdims=True) * (1.0 / D)))


def head_pairs(body):
    def step(i, _):
        seq = i // 3
        pair = i - seq * 3
        rows = pl.ds(pl.multiple_of(seq * SEQ, SEQ), SEQ)
        body(i, rows, pair)
        return 0
    lax.fori_loop(0, 6, step, 0)


def pair_cols(which, pair):
    return pl.ds(pl.multiple_of(which * D + pair * 128, 128), 128)


def attn_forward(x_ref, ln_ref, wqkv_ref, qkv_s, p_s, o_s):
    def qkv_tile(rows):
        normed, _ = ln_norm(x_ref[rows, :].astype(F32))
        a_in = (normed * ln_ref[0:1, :] + ln_ref[1:2, :]).astype(BF16)
        qkv_s[rows, :] = dot_nn(a_in, wqkv_ref[...]).astype(BF16)
    row_tiles(qkv_tile)

    def heads(i, rows, pair):
        q2 = qkv_s[rows, pair_cols(0, pair)]
        k2 = qkv_s[rows, pair_cols(1, pair)]
        v2 = qkv_s[rows, pair_cols(2, pair)]
        outs = []
        for e in range(2):
            cut = slice(e * 64, e * 64 + 64)
            scores = dot_nt(q2[:, cut], k2[:, cut]) * 0.125
            top = jnp.max(scores, axis=-1, keepdims=True)
            expd = jnp.exp(scores - top)
            total = jnp.sum(expd, axis=-1, keepdims=True)
            probs = (expd * (1.0 / total)).astype(BF16)
            p_s[i * 2 + e] = probs
            outs.append(dot_nn(probs, v2[:, cut]).astype(BF16))
        o_s[rows, pair_cols(0, pair)] = jnp.concatenate(outs, axis=1)
    head_pairs(heads)


def hidden(x_ref, o_s, wout_ref, h_s, rows):
    hid = (x_ref[rows, :].astype(F32) + dot_nn(o_s[rows, :], wout_ref[...])).astype(BF16)
    h_s[rows, :] = hid
    return hid.astype(F32)


def gelu_parts(up):
    up2 = up * up
    tanh = jnp.tanh(GELU_C * up * (1.0 + GELU_A * up2))
    half = 0.5 + 0.5 * tanh
    return up2, tanh, half


def mlp_forward(hid32, ln_ref, wup_ref, wdown_ref):
    normed, _ = ln_norm(hid32)
    m_in = (normed * ln_ref[2:3, :] + ln_ref[3:4, :]).astype(BF16)
    total = None
    for c in range(4):
        up = dot_nn(m_in, wup_ref[:, c * D:(c + 1) * D])
        act = (up * gelu_parts(up)[2]).astype(BF16)
        part = dot_nn(act, wdown_ref[c * D:(c + 1) * D, :])
        total = part if total is None else total + part
    return (hid32 + total).astype(BF16)


def mlp_backward(hid32, dy, ln_ref, wup_ref, wout_ref, wdown_ref, m_s, act_s, dup_s, dhid_s, datt_s, lng_ref, rows, emit):
    normed, inv_std = ln_norm(hid32)
    m_in = (normed * ln_ref[2:3, :] + ln_ref[3:4, :]).astype(BF16)
    m_s[rows, :] = m_in
    total = None
    dm = None
    for c in range(4):
        cols = slice(c * D, (c + 1) * D)
        up = dot_nn(m_in, wup_ref[:, cols])
        up2, tanh, half = gelu_parts(up)
        act = (up * half).astype(BF16)
        act_s[rows, cols] = act
        if emit is not None:
            part = dot_nn(act, wdown_ref[cols, :])
            total = part if total is None else total + part
        slope = half + (0.5 * up) * (1.0 - tanh * tanh) * (GELU_C + (3.0 * GELU_A * GELU_C) * up2)
        d_act = dot_nt(dy, wdown_ref[cols, :]).astype(BF16).astype(F32)
        d_up = (d_act * slope).astype(BF16)
        dup_s[rows, cols] = d_up
        d_part = dot_nt(d_up, wup_ref[:, cols])
        dm = d_part if dm is None else dm + d_part
    if emit is not None:
        emit[rows, :] = (hid32 + total).astype(BF16)
    dm32 = dm.astype(BF16).astype(F32)
    lng_ref[2:3, :] += jnp.sum(dm32 * normed, axis=0, keepdims=True)
    lng_ref[3:4, :] += jnp.sum(dm32, axis=0, keepdims=True)
    d_hid32 = ln_back(dm32, normed, inv_std, ln_ref[2:3, :])
    d_hid = (d_hid32 + dy.astype(F32)).astype(BF16)
    dhid_s[rows, :] = d_hid
    datt_s[rows, :] = dot_nt(d_hid, wout_ref[...]).astype(BF16)


def mlp_grads(g_ref, m_s, act_s, dup_s, dhid_s, o_s, dy_ref):
    def chunk(c, _):
        cols = pl.ds(pl.multiple_of(c * D, D), D)
        g_ref[4 + c] = dot_tn(m_s[...], dup_s[:, cols])
        g_ref[8 + c] = dot_tn(act_s[:, cols], dy_ref[...])
        return 0
    lax.fori_loop(0, 4, chunk, 0)
    g_ref[3] = dot_tn(o_s[...], dhid_s[...])


def attn_backward(qkv_s, p_s, datt_s, dqkv_s):
    def heads(i, rows, pair):
        q2 = qkv_s[rows, pair_cols(0, pair)]
        k2 = qkv_s[rows, pair_cols(1, pair)]
        v2 = qkv_s[rows, pair_cols(2, pair)]
        do2 = datt_s[rows, pair_cols(0, pair)]
        dqs, dks, dvs = [], [], []
        for e in range(2):
            cut = slice(e * 64, e * 64 + 64)
            probs = p_s[i * 2 + e]
            d_out = do2[:, cut]
            d_probs = dot_nt(d_out, v2[:, cut]).astype(BF16).astype(F32)
            p32 = probs.astype(F32)
            row_dot = jnp.sum(d_probs * p32, axis=-1, keepdims=True)
            d_scores = (p32 * (d_probs - row_dot) * 0.125).astype(BF16)
            dqs.append(dot_nn(d_scores, k2[:, cut]).astype(BF16))
            dks.append(dot_tn(d_scores, q2[:, cut]).astype(BF16))
            dvs.append(dot_tn(probs, d_out).astype(BF16))
        dqkv_s[rows, pair_cols(0, pair)] = jnp.concatenate(dqs, axis=1)
        dqkv_s[rows, pair_cols(1, pair)] = jnp.concatenate(dks, axis=1)
        dqkv_s[rows, pair_cols(2, pair)] = jnp.concatenate(dvs, axis=1)
    head_pairs(heads)


def qkv_backward(x_ref, dqkv_s, dhid_s, ln_ref, wqkv_ref, a_s, dx_ref, lng_ref):
    def tile(rows):
        normed, inv_std = ln_norm(x_ref[rows, :].astype(F32))
        a_s[rows, :] = (normed * ln_ref[0:1, :] + ln_ref[1:2, :]).astype(BF16)
        da32 = dot_nt(dqkv_s[rows, :], wqkv_ref[...]).astype(BF16).astype(F32)
        lng_ref[0:1, :] += jnp.sum(da32 * normed, axis=0, keepdims=True)
        lng_ref[1:2, :] += jnp.sum(da32, axis=0, keepdims=True)
        d_in = ln_back(da32, normed, inv_std, ln_ref[0:1, :])
        dx_ref[rows, :] = (d_in + dhid_s[rows, :].astype(F32)).astype(BF16)
    row_tiles(tile)


def qkv_grads(g_ref, a_s, dqkv_s):
    def chunk(c, _):
        g_ref[c] = dot_tn(a_s[...], dqkv_s[:, pl.ds(pl.multiple_of(c * D, D), D)])
        return 0
    lax.fori_loop(0, 3, chunk, 0)


def spatial_forward_kernel(x_ref, ln_ref, wqkv_ref, wout_ref, wup_ref, wdown_ref, mid_ref, qkv_s, p_s, o_s, h_s):
    attn_forward(x_ref, ln_ref, wqkv_ref, qkv_s, p_s, o_s)

    def tail(rows):
        hid32 = hidden(x_ref, o_s, wout_ref, h_s, rows)
        mid_ref[rows, :] = mlp_forward(hid32, ln_ref, wup_ref, wdown_ref)
    row_tiles(tail)


def temporal_kernel(x_ref, dy_ref, ln_ref, wqkv_ref, wout_ref, wup_ref, wdown_ref, out_ref, dx_ref, g_ref, lng_ref,
                    qkv_s, p_s, o_s, h_s, m_s, act_s, dup_s, dhid_s, datt_s, dqkv_s, a_s):
    lng_ref[...] = jnp.zeros_like(lng_ref)
    attn_forward(x_ref, ln_ref, wqkv_ref, qkv_s, p_s, o_s)

    def tail(rows):
        hid32 = hidden(x_ref, o_s, wout_ref, h_s, rows)
        mlp_backward(hid32, dy_ref[rows, :], ln_ref, wup_ref, wout_ref, wdown_ref, m_s, act_s, dup_s, dhid_s, datt_s,
                     lng_ref, rows, out_ref)
    row_tiles(tail)
    attn_backward(qkv_s, p_s, datt_s, dqkv_s)
    qkv_backward(x_ref, dqkv_s, dhid_s, ln_ref, wqkv_ref, a_s, dx_ref, lng_ref)
    mlp_grads(g_ref, m_s, act_s, dup_s, dhid_s, o_s, dy_ref)
    qkv_grads(g_ref, a_s, dqkv_s)


def spatial_backward_kernel(x_ref, dy_ref, qkv_s, p_s, o_s, h_s, ln_ref, wqkv_ref, wout_ref, wup_ref, wdown_ref,
                            dx_ref, g_ref, lng_ref, m_s, act_s, dup_s, dhid_s, datt_s, dqkv_s, a_s):
    lng_ref[...] = jnp.zeros_like(lng_ref)

    def tail(rows):
        mlp_backward(h_s[rows, :].astype(F32), dy_ref[rows, :], ln_ref, wup_ref, wout_ref, wdown_ref, m_s, act_s, dup_s,
                     dhid_s, datt_s, lng_ref, rows, None)
    row_tiles(tail)
    mlp_grads(g_ref, m_s, act_s, dup_s, dhid_s, o_s, dy_ref)
    attn_backward(qkv_s, p_s, datt_s, dqkv_s)
    qkv_backward(x_ref, dqkv_s, dhid_s, ln_ref, wqkv_ref, a_s, dx_ref, lng_ref)
    qkv_grads(g_ref, a_s, dqkv_s)


def vmem_spec():
    return pl.BlockSpec(memory_space=pltpu.VMEM)


def call_kernel(kernel, args, outs, scratch, flops):
    return pl.pallas_call(
        kernel,
        out_shape=[jax.ShapeDtypeStruct(s, t) for s, t in outs],
        in_specs=[vmem_spec()] * len(args),
        out_specs=[vmem_spec()] * len(outs),
        scratch_shapes=[pltpu.VMEM(s, t) for s, t in scratch],
        compiler_params=pltpu.CompilerParams(vmem_limit_bytes=VMEM_LIMIT),
        cost_estimate=pl.CostEstimate(flops=flops, bytes_accessed=10_000_000, transcendentals=0),
    )(*args)


ACT = ((T, D), BF16)
QKV = ((T, 3 * D), BF16)
PROBS = ((12, SEQ, SEQ), BF16)
WIDE = ((T, FF), BF16)
GRAD = ((12, D, D), F32)
LNG = ((8, D), F32)
BACK_SCRATCH = [ACT, WIDE, WIDE, ACT, ACT, QKV, ACT]


def swap_kernel(n, src_ref, dst_ref, send_sem, recv_sem, local_sem):
    me = lax.axis_index("sp")
    mine = pltpu.make_async_copy(src_ref.at[me], dst_ref.at[me], local_sem)
    mine.start()

    def remote(k):
        to = lax.rem(me + k, n)
        return pltpu.make_async_remote_copy(src_ref.at[to], dst_ref.at[me], send_sem, recv_sem,
                                            device_id={"sp": to}, device_id_type=MESH)

    def start(k, _):
        remote(k).start()
        return 0
    lax.fori_loop(1, n, start, 0)
    mine.wait()
    whole = pltpu.make_async_copy(src_ref.at[pl.ds(0, n - 1)], dst_ref.at[pl.ds(0, n - 1)], send_sem)
    whole.wait()
    whole = pltpu.make_async_copy(src_ref.at[pl.ds(0, n - 1)], dst_ref.at[pl.ds(0, n - 1)], recv_sem)
    whole.wait()


def swap(n, pieces):
    return pl.pallas_call(
        functools.partial(swap_kernel, n),
        out_shape=jax.ShapeDtypeStruct(pieces.shape, pieces.dtype),
        in_specs=[vmem_spec()],
        out_specs=vmem_spec(),
        scratch_shapes=[pltpu.SemaphoreType.DMA] * 3,
        compiler_params=pltpu.CompilerParams(has_side_effects=True),
    )(pieces)


SIZES = (192, 96, 48, 24, 24, 24)
RECV_OFF = (0, 192, 288, 336, 360, 384)
RECV_ROWS = 408


def dim_info(me, dim):
    axis, far = dim // 2, dim % 2
    stride = (2, 8, 32)[axis]
    coord = lax.rem(lax.div(me, stride), 4)
    if far:
        bit = lax.div(coord, 2)
        partner = me + (3 - 2 * coord) * stride
    else:
        bit = lax.rem(coord + lax.div(coord, 2), 2)
        partner = me + (1 - 2 * lax.rem(coord, 2)) * stride
    return bit, partner


def reduce_kernel(g0_ref, g1_ref, ln_ref, o0_ref, o1_ref, oln_ref, acc, half, recv, lnacc, lnrecv,
                  half_send, half_recv, load_sem, send_sem, recv_sem, back_send, back_recv, out_send, out_recv, out_local,
                  ln_send, ln_recv, free_sem):
    me = lax.axis_index("sp")
    core = lax.rem(me, 2)
    sibling = me + 1 - 2 * core
    grads = (g0_ref, g1_ref)
    outs = (o0_ref, o1_ref)
    dims = [dim_info(me, d) for d in range(6)]

    def remote(src, dst, s_sem, r_sem, to):
        return pltpu.make_async_remote_copy(src, dst, s_sem, r_sem, device_id={"sp": to}, device_id_type=MESH)

    halves = {}
    loads = {}
    for p in range(6):
        for b in range(2):
            halves[b, p] = remote(grads[b].at[6 * (1 - core) + p], half.at[b, p], half_send.at[b, p], half_recv.at[b, p], sibling)
            halves[b, p].start()
            loads[b, p] = pltpu.make_async_copy(grads[b].at[6 * core + p], acc.at[b, p], load_sem.at[b, p])
            loads[b, p].start()

    lnacc[...] = ln_ref[...]
    ln_copies = []

    def ln_start(t):
        to = sibling if t == 0 else dims[t - 1][1]
        copy = remote(lnacc, lnrecv.at[t], ln_send.at[t], ln_recv.at[t], to)
        copy.start()
        ln_copies.append(copy)

    def ln_finish(t):
        ln_copies[t].wait()
        lnacc[...] += lnrecv[t]

    ln_start(0)

    offs = {}
    sends = {}

    def start_send(t, p, b):
        dim = (p + t) % 6
        bit, partner = dims[dim]
        off = offs[p, t]
        size = SIZES[t]
        if t < 4:
            keep = off + bit * size
            give = off + (1 - bit) * size
        else:
            keep = give = off
        offs[p, t + 1] = keep
        copy = remote(acc.at[b, p, pl.ds(pl.multiple_of(give, 8), size)], recv.at[b, p, pl.ds(RECV_OFF[t], size)],
                      send_sem.at[t, b, p], recv_sem.at[t, b, p], partner)
        copy.start()
        sends[t, p, b] = copy

    for p in range(6):
        offs[p, 0] = jnp.int32(0)
        for b in range(2):
            halves[b, p].wait()
            loads[b, p].wait()
            acc[b, p] += half[b, p]
            start_send(0, p, b)
    ln_finish(0)
    ln_start(1)
    backs = {}
    finals = []

    def forward(b, p, off, size, slot):
        rows = pl.ds(pl.multiple_of(off, 8), size)
        copy = remote(acc.at[b, p, rows], outs[b].at[6 * core + p, rows], out_send.at[slot, b, p], out_recv.at[slot, b, p], sibling)
        copy.start()
        finals.append(copy)
        copy = pltpu.make_async_copy(acc.at[b, p, rows], outs[b].at[6 * core + p, rows], out_local.at[slot, b, p])
        copy.start()
        finals.append(copy)

    def start_back(t, p, b):
        dim = (p + t) % 6
        _, partner = dims[dim]
        pl.semaphore_wait(free_sem.at[t, b, p], 1)
        rows = pl.ds(pl.multiple_of(offs[p, t + 1], 8), SIZES[t])
        copy = remote(acc.at[b, p, rows], acc.at[b, p, rows], back_send.at[t, b, p], back_recv.at[t, b, p], partner)
        copy.start()
        backs[t, p, b] = copy

    for t in range(6):
        for p in range(6):
            for b in range(2):
                sends[t, p, b].wait()
                if t < 4:
                    pl.semaphore_signal(free_sem.at[t, b, p], inc=1, device_id={"sp": dims[(p + t) % 6][1]}, device_id_type=MESH)
                size = SIZES[t]
                rows = pl.ds(pl.multiple_of(offs[p, t + 1], 8), size)
                acc[b, p, rows] += recv[b, p, pl.ds(RECV_OFF[t], size)]
                if t < 5:
                    start_send(t + 1, p, b)
                else:
                    start_back(3, p, b)
                    forward(b, p, offs[p, 4], 24, 0)
        ln_finish(t + 1)
        if t < 5:
            ln_start(t + 2)
    oln_ref[...] = lnacc[...]
    for t in (3, 2, 1, 0):
        for p in range(6):
            for b in range(2):
                backs[t, p, b].wait()
                if t > 0:
                    start_back(t - 1, p, b)
                bit = dims[(p + t) % 6][0]
                size = SIZES[t]
                forward(b, p, offs[p, t + 1] + (1 - 2 * bit) * size, size, 4 - t)
    for copy in finals:
        copy.wait()


def reduce_grads(g0, g1, ln):
    dma = pltpu.SemaphoreType.DMA
    any_spec = pl.BlockSpec(memory_space=pl.ANY)
    return pl.pallas_call(
        reduce_kernel,
        out_shape=[jax.ShapeDtypeStruct(g0.shape, F32), jax.ShapeDtypeStruct(g1.shape, F32), jax.ShapeDtypeStruct(ln.shape, F32)],
        in_specs=[any_spec, any_spec, vmem_spec()],
        out_specs=[any_spec, any_spec, vmem_spec()],
        scratch_shapes=[
            pltpu.VMEM((2, 6, D, D), F32), pltpu.VMEM((2, 6, D, D), F32), pltpu.VMEM((2, 6, RECV_ROWS, D), F32),
            pltpu.VMEM(ln.shape, F32), pltpu.VMEM((7,) + ln.shape, F32),
            dma((2, 6)), dma((2, 6)), dma((2, 6)), dma((6, 2, 6)), dma((6, 2, 6)), dma((4, 2, 6)), dma((4, 2, 6)),
            dma((5, 2, 6)), dma((5, 2, 6)), dma((5, 2, 6)), dma((7,)), dma((7,)),
            pltpu.SemaphoreType.REGULAR((4, 2, 6)),
        ],
        compiler_params=pltpu.CompilerParams(has_side_effects=True, vmem_limit_bytes=VMEM_LIMIT),
    )(g0, g1, ln)


def to_pieces(act, n):
    return act.reshape(2, n, 2, D).transpose(1, 0, 2, 3).reshape(n, 4, D)


def from_pieces(pieces, n):
    return pieces.reshape(n, 2, 2, D).transpose(2, 0, 1, 3).reshape(T, D)


def device_step(n, latents, cotangent, ln_params, w_qkv, w_out, w_up, w_down):
    ln32 = ln_params.astype(F32)
    weights = [(ln32[i], w_qkv[i], w_out[i].reshape(D, D), w_up[i], w_down[i]) for i in range(2)]
    x = latents.reshape(T, D)
    cot = from_pieces(swap(n, to_pieces(cotangent.reshape(T, D), n)), n)
    mid, qkv, probs, attn, hid = call_kernel(spatial_forward_kernel, (x,) + weights[0], [ACT, QKV, PROBS, ACT, ACT], [], 2_000_000_000)
    mid_t = from_pieces(swap(n, to_pieces(mid, n)), n)
    out, d_mid_t, g1, lng1 = call_kernel(temporal_kernel, (mid_t, cot) + weights[1], [ACT, ACT, GRAD, LNG],
                                         [QKV, PROBS, ACT, ACT] + BACK_SCRATCH, 6_000_000_000)
    d_mid = from_pieces(swap(n, to_pieces(d_mid_t, n)), n)
    result = from_pieces(swap(n, to_pieces(out, n)), n)
    dx, g0, lng0 = call_kernel(spatial_backward_kernel, (x, d_mid, qkv, probs, attn, hid) + weights[0], [ACT, GRAD, LNG],
                               BACK_SCRATCH, 4_000_000_000)
    r0, r1, rln = reduce_grads(g0, g1, jnp.concatenate([lng0, lng1], axis=0))
    blocks = jnp.stack([r0, r1])

    def wide(first, count):
        return blocks[:, first:first + count].transpose(0, 2, 1, 3).reshape(2, D, count * D)
    ln_grad = rln.reshape(2, 8, D)[:, :4]
    return (result.reshape(latents.shape), dx.reshape(latents.shape), ln_grad, wide(0, 3), blocks[:, 3].reshape(2, 6, 64, D),
            wide(4, 4), blocks[:, 8:12].reshape(2, FF, D))


def solution(mesh):
    act_spec = P('data', 'sp', None, None)
    replicated = P()
    part_spec = P('data')
    return jax.shard_map(functools.partial(device_step, mesh.shape["sp"]), mesh=mesh,
                         in_specs=(act_spec, act_spec, replicated, replicated, replicated, replicated, replicated),
                         out_specs=(act_spec, act_spec, part_spec, part_spec, part_spec, part_spec, part_spec),
                         check_vma=False)
```

time: 389 us -> 312 us (0.80); the launches traced: 381 us -> 312 us
  Pallas kernels: 0 us -> 252 us
  waiting for transfers between devices: 106 us -> 0 us
  matrix products: 72 us -> 0 us
  blocking collectives: 63.6 us -> 0 us
  starting transfers between devices: 32.3 us -> 0 us
  other arithmetic: 39 us -> 10.5 us
  between operations: 15.3 us -> 0.8 us
  local copies, waits for them, and re-layouts: 53.1 us -> 48.5 us
    pallas_call x0 -> x8, Pallas kernels: none -> 252 us  [the longest x1 93 us: reduce_grads(): pl.pallas_call(reduce_kernel, out_shape=[jax.ShapeDtypeStruct(g0.shape, F...]
    psum x1 -> x0, waiting for transfers between devices: 79.7 us -> none  [device_step(): lax.psum([jnp.stack([grad_s, grad_t]) for grad_s, grad_t in zip(spatial_g...]
    dot_general x36 -> x0, matrix products: 72 us -> none  [the longest x2 8.85 us: attend_backward(): jnp.einsum(attn_forms[2], d_scores, qkv_heads[0], preferred_element_type=...]
    psum x1 -> x0, blocking collectives: 63.6 us -> none  [device_step(): lax.psum([jnp.stack([grad_s, grad_t]) for grad_s, grad_t in zip(spatial_g...]
    all_to_all x4 -> x0, starting transfers between devices: 32.1 us -> none  [the longest x1 11.5 us: device_step(): mid_swap = lax.all_to_all(mid_act, 'sp', 2, 1, tiled=True)]
    all_to_all x4 -> x0, waiting for transfers between devices: 26.6 us -> none  [the longest x1 14 us: device_step(): result = lax.all_to_all(out_swap, 'sp', 1, 2, tiled=True)]
    reshape x0 -> x20, local copies, waits for them, and re-layouts: none -> 15.3 us  [the longest x10 8.31 us: from_pieces(): return pieces.reshape(n, 2, 2, D).transpose(2, 0, 1, 3).reshape(T, D)]
    transpose x0 -> x2, local copies, waits for them, and re-layouts: none -> 9.4 us  [wide(): blocks[:, first:first + count].transpose(0, 2, 1, 3)]
  transfers between devices with their start and end apart: 5 -> 0, of which waited for: 4 -> 0; matrix products, arithmetic and copies ran while one was open for 10% -> 0% of each run, Pallas kernels for 0% -> 0%
where the time goes in v1:
time: 312 us
  Pallas kernels  252 us (81%)
  local copies, waits for them, and re-layouts  48.5 us (16%)
  other arithmetic  10.5 us (3%)
    pallas_call x1, Pallas kernels, reduce_grads(): pl.pallas_call(reduce_kernel, out_shape=[jax.ShapeDtypeStruct(g0.shape, F...  93 us
    pallas_call x3, Pallas kernels, call_kernel(): pl.pallas_call(kernel, out_shape=[jax.ShapeDtypeStruct(s, t) for s, t in...  79.6 us
    pallas_call x4, Pallas kernels, swap(): pl.pallas_call(functools.partial(swap_kernel, n), out_shape=jax.ShapeDtyp...  79.1 us
    unnamed x16, local copies, waits for them, and re-layouts  11.3 us
    transpose x2, local copies, waits for them, and re-layouts, wide(): blocks[:, first:first + count].transpose(0, 2, 1, 3)  9.4 us
    reshape x10, local copies, waits for them, and re-layouts, from_pieces(): return pieces.reshape(n, 2, 2, D).transpose(2, 0, 1, 3).reshape(T, D)  8.31 us
    reshape x10, local copies, waits for them, and re-layouts, to_pieces(): return act.reshape(2, n, 2, D).transpose(1, 0, 2, 3).reshape(n, 4, D)  7.03 us
    another operation x2, other arithmetic, device_step(): blocks = jnp.stack([r0, r1])  6.45 us

profile of v1, /device:TPU:1, one launch (start us, length us, event | category | flops | bytes accessed | tf_op | source)
XLA Modules:
  0.0 311.5 jit_solution(4230903381163241848)
XLA Ops:
  0.6 0.7 convert_element_type.3
  1.3 0.6 slice_bitcast_fusion.6
  1.9 1.1 reshape_reshape.6
  3.1 0.0 copy-start.1
  3.1 0.3 copy.46
  3.4 0.9 reshape.79.src_ref
  4.3 24.0 %shard_map.128 = bf16[128,4,384]{2,1,0:T(4,128)(2,1)} custom-call(bf16[128,4,384]{2,1,0:T(4,128)(2,1)} %reshape.79.src_ref), custom_call_target="tpu_custom_call" | custom-call | tf_op jit(solution)/shard_map/pallas_call | solution.py:290
  28.3 1.2 reshape.80
  29.5 0.3 copy.45
  29.8 0.9 reshape.81.dy_ref
  30.7 2.1 fusion.5
  32.8 2.8 slice_bitcast_fusion.4
  35.6 1.6 slice_bitcast_fusion.1
  37.1 1.6 slice_bitcast_fusion
  38.8 16.6 %shard_map.126 = (bf16[512,384]{1,0:T(8,128)(2,1)}, bf16[512,1152]{1,0:T(8,128)(2,1)}, bf16[12,256,256]{2,1,0:T(8,128)(2,1)}, bf16[512,384]{1,0:T(8,128)(2,1)}, bf16[512,384]{1,0:T(8,128)(2,1)}) custom-call(bf16[512,384]{1,0:T(8,128)(2,1)} %bitcast.81, f32[4,384]{1,0:T(4,128)} %get-tuple-element.55.ln_ref, bf16[384,1152]{1,0:T(8,128)(2,1)} %get-tuple-element.51.wqkv_ref, ...), custom_call_target="tpu_custom_call" | custom-call | flops 2000000000 | bytes 10000000 | tf_op jit(solution)/shard_map/pallas_call | solution.py:248
  55.3 1.1 reshape.75
  56.5 0.3 copy.48
  56.8 0.9 reshape.76.src_ref
  57.7 18.4 %shard_map.127 = bf16[128,4,384]{2,1,0:T(4,128)(2,1)} custom-call(bf16[128,4,384]{2,1,0:T(4,128)(2,1)} %reshape.76.src_ref), custom_call_target="tpu_custom_call" | custom-call | tf_op jit(solution)/shard_map/pallas_call | solution.py:290
  76.2 1.2 reshape.77
  77.3 0.3 copy.47
  77.7 0.9 reshape.78.x_ref
  78.5 36.5 %shard_map.129 = (bf16[512,384]{1,0:T(8,128)(2,1)}, bf16[512,384]{1,0:T(8,128)(2,1)}, f32[12,384,384]{2,1,0:T(8,128)}, f32[8,384]{1,0:T(8,128)}) custom-call(bf16[512,384]{1,0:T(8,128)(2,1)} %reshape.78.x_ref, bf16[512,384]{1,0:T(8,128)(2,1)} %reshape.81.dy_ref, f32[4,384]{1,0:T(4,128)} %get-tuple-element.54.ln_ref, ...), custom_call_target="tpu_custom_call" | custom-call | flops 6000000000 | bytes 10000000 | tf_op jit(solution)/shard_map/pallas_call | solution.py:248
  115.1 1.2 reshape.82
  116.3 0.3 copy.44
  116.6 0.9 reshape.83.src_ref
  117.5 18.4 %shard_map.130 = bf16[128,4,384]{2,1,0:T(4,128)(2,1)} custom-call(bf16[128,4,384]{2,1,0:T(4,128)(2,1)} %reshape.83.src_ref), custom_call_target="tpu_custom_call" | custom-call | tf_op jit(solution)/shard_map/pallas_call | solution.py:290
  135.9 1.2 reshape.84
  137.1 0.8 copy.34
  137.9 0.1 reshape.85
  138.0 0.3 copy.43
  138.3 0.9 reshape.86.src_ref
  139.2 18.4 %shard_map.131 = bf16[128,4,384]{2,1,0:T(4,128)(2,1)} custom-call(bf16[128,4,384]{2,1,0:T(4,128)(2,1)} %reshape.86.src_ref), custom_call_target="tpu_custom_call" | custom-call | tf_op jit(solution)/shard_map/pallas_call | solution.py:290
  157.6 1.2 reshape.87
  158.8 0.3 copy.42
  159.1 0.9 reshape.88.dy_ref
  160.0 26.5 %shard_map.132 = (bf16[512,384]{1,0:T(8,128)(2,1)}, f32[12,384,384]{2,1,0:T(8,128)}, f32[8,384]{1,0:T(8,128)}) custom-call(bf16[512,384]{1,0:T(8,128)(2,1)} %bitcast.82, bf16[512,384]{1,0:T(8,128)(2,1)} %reshape.88.dy_ref, bf16[512,1152]{1,0:T(8,128)(2,1)} %get-tuple-element.25.qkv_s, bf16[12,256,256]{2,1,0:T(8,128)(2,1)} %get-tuple-element.26.p_s, ...), custom_call_target="tpu_custom_call" | custom-call | flops 4000000000 | bytes 10000000 | tf_op jit(solution)/shard_map/pallas_call | solution.py:248
  186.5 1.3 pad_maximum_fusion.1.ln_ref
  187.8 93.0 %shard_map.133 = (f32[12,384,384]{2,1,0:T(8,128)}, f32[12,384,384]{2,1,0:T(8,128)}, f32[16,384]{1,0:T(8,128)}) custom-call(f32[12,384,384]{2,1,0:T(8,128)} %get-tuple-element.30.g0_ref, f32[12,384,384]{2,1,0:T(8,128)} %get-tuple-element.31.g1_ref, f32[16,384]{1,0:T(8,128)} %pad_maximum_fusion.1.ln_ref), custom_call_target="tpu_custom_call" | custom-call | tf_op jit(solution)/shard_map/pallas_call | solution.py:438
  280.8 1.5 slice.62
  282.3 2.5 fusion.4
  284.8 2.3 copy-done
  287.1 2.0 fusion.3
  289.1 4.0 %pad_maximum_fusion = (f32[2,4,384,384]{3,2,1,0:T(8,128)}, f32[2,384,4,384]{3,1,2,0:T(8,128)}) fusion(f32[1,12,384,384]{3,2,1,0:T(8,128)S(1)} %bitcast.64, f32[1,12,384,384]{3,2,1,0:T(8,128)S(1)} %bitcast.61), kind=kLoop, calls=%fused_computation.8 | loop fusion | flops 2359296 | bytes 23592960 | tf_op jit(solution)/shard_map/stack | solution.py:476
  293.1 3.3 %copy.30 = f32[2,384,3,384]{1,3,2,0:T(8,128)S(1)} copy(f32[2,384,3,384]{3,1,2,0:T(8,128)} %fusion.3) | data formatting | bytes 7077888 | tf_op jit(solution)/shard_map/transpose | solution.py:479
  296.4 2.9 copy.32
  299.4 6.1 %copy.31 = f32[2,384,4,384]{1,3,2,0:T(8,128)} copy(f32[2,384,4,384]{3,1,2,0:T(8,128)} %get-tuple-element.45) | data formatting | bytes 9437184 | tf_op jit(solution)/shard_map/transpose | solution.py:479
  305.5 6.0 %copy.33 = f32[2,384,1536]{2,1,0:T(8,128)} copy(f32[2,384,1536]{1,2,0:T(8,128)} %bitcast.65) | data formatting | bytes 9437184
  (13 shorter events, 0.0 us)
Async XLA Ops:
  3.1 32.5 %copy-start.1 = (bf16[2,384,1536]{2,1,0:T(8,128)(2,1)S(1)}, bf16[2,384,1536]{2,1,0:T(8,128)(2,1)}, u32[]{:S(2)}) copy-start(bf16[2,384,1536]{2,1,0:T(8,128)(2,1)} %param.12) | copy-start | bytes 7077892
  30.7 6.5 %copy-start.2 = (bf16[2,1536,384]{2,1,0:T(8,128)(2,1)S(1)}, bf16[2,1536,384]{2,1,0:T(8,128)(2,1)}, u32[]{:S(2)}) copy-start(bf16[2,1536,384]{2,1,0:T(8,128)(2,1)} %param.13) | copy-start | bytes 7077892
  115.1 22.8 %copy-start.3 = (bf16[512,384]{1,0:T(8,128)(2,1)S(1)}, bf16[512,384]{1,0:T(8,128)(2,1)}, u32[]{:S(2)}) copy-start(bf16[512,384]{1,0:T(8,128)(2,1)} %get-tuple-element.24) | copy-start | bytes 1179652
  160.0 26.5 %copy-start.4 = (f32[8,384]{1,0:T(8,128)S(1)}, f32[8,384]{1,0:T(8,128)}, u32[]{:S(2)}) copy-start(f32[8,384]{1,0:T(8,128)} %get-tuple-element.33) | copy-start | bytes 36868
  280.8 4.0 %slice-start = ((s8[7077888]{0:T(1024)(128)(4,1)}), s8[4194304]{0:T(1024)(128)(4,1)S(1)}, s32[]{:S(2)}) async-start(s8[7077888]{0:T(1024)(128)(4,1)} %bitcast.58), calls=%async_computation | async-start | bytes 8388608
  282.3 2.5 slice-start.1
  282.3 4.8 %copy-start = (f32[12,384,384]{2,1,0:T(8,128)S(1)}, f32[12,384,384]{2,1,0:T(8,128)}, u32[]{:S(2)}) copy-start(f32[12,384,384]{2,1,0:T(8,128)} %get-tuple-element.36) | copy-start | bytes 21233668

commit v2 on v1

v2 whole, which is shorter than its diff:
```python
import functools

import jax
import jax.numpy as jnp
from jax import lax
from jax.experimental import pallas as pl
from jax.experimental.pallas import tpu as pltpu
from jax.sharding import PartitionSpec as P

F32 = jnp.float32
BF16 = jnp.bfloat16
D = 384
T = 512
SEQ = 256
FF = 1536
ROWS = 128
MESH = pl.DeviceIdType.MESH
VMEM_LIMIT = 60 * 1024 * 1024
GELU_C = 0.7978845608028654
GELU_A = 0.044715


def dot_nn(a, b):
    return lax.dot_general(a, b, (((1,), (0,)), ((), ())), preferred_element_type=F32)


def dot_nt(a, b):
    return lax.dot_general(a, b, (((1,), (1,)), ((), ())), preferred_element_type=F32)


def dot_tn(a, b):
    return lax.dot_general(a, b, (((0,), (0,)), ((), ())), preferred_element_type=F32)


def row_tiles(body, first=0, last=T // ROWS):
    def step(i, _):
        body(pl.ds(pl.multiple_of(i * ROWS, ROWS), ROWS))
        return 0
    lax.fori_loop(first, last, step, 0)


def ln_norm(x32):
    mean = jnp.sum(x32, axis=-1, keepdims=True) * (1.0 / D)
    centered = x32 - mean
    inv_std = lax.rsqrt(jnp.sum(centered * centered, axis=-1, keepdims=True) * (1.0 / D) + 1e-6)
    return centered * inv_std, inv_std


def ln_back(d32, normed, inv_std, gain):
    d_norm = d32 * gain
    d_center = d_norm - jnp.sum(d_norm, axis=-1, keepdims=True) * (1.0 / D)
    return inv_std * (d_center - normed * (jnp.sum(d_norm * normed, axis=-1, keepdims=True) * (1.0 / D)))


def head_pairs(body, first=0, last=6):
    def step(i, _):
        seq = i // 3
        pair = i - seq * 3
        rows = pl.ds(pl.multiple_of(seq * SEQ, SEQ), SEQ)
        body(i, rows, pair)
        return 0
    lax.fori_loop(first, last, step, 0)


def pair_cols(which, pair):
    return pl.ds(pl.multiple_of(which * D + pair * 128, 128), 128)


def attn_forward(x_ref, ln_ref, wqkv_ref, qkv_s, p_s, o_s):
    def qkv_tile(rows):
        normed, _ = ln_norm(x_ref[rows, :].astype(F32))
        a_in = (normed * ln_ref[0:1, :] + ln_ref[1:2, :]).astype(BF16)
        qkv_s[rows, :] = dot_nn(a_in, wqkv_ref[...]).astype(BF16)
    row_tiles(qkv_tile)

    def heads(i, rows, pair):
        q2 = qkv_s[rows, pair_cols(0, pair)]
        k2 = qkv_s[rows, pair_cols(1, pair)]
        v2 = qkv_s[rows, pair_cols(2, pair)]
        outs = []
        for e in range(2):
            cut = slice(e * 64, e * 64 + 64)
            scores = dot_nt(q2[:, cut], k2[:, cut]) * 0.125
            top = jnp.max(scores, axis=-1, keepdims=True)
            expd = jnp.exp(scores - top)
            total = jnp.sum(expd, axis=-1, keepdims=True)
            probs = (expd * (1.0 / total)).astype(BF16)
            p_s[i * 2 + e] = probs
            outs.append(dot_nn(probs, v2[:, cut]).astype(BF16))
        o_s[rows, pair_cols(0, pair)] = jnp.concatenate(outs, axis=1)
    head_pairs(heads)


def hidden(x_ref, o_s, wout_ref, h_s, rows):
    hid = (x_ref[rows, :].astype(F32) + dot_nn(o_s[rows, :], wout_ref[...])).astype(BF16)
    h_s[rows, :] = hid
    return hid.astype(F32)


def gelu_parts(up):
    up2 = up * up
    tanh = jnp.tanh(GELU_C * up * (1.0 + GELU_A * up2))
    half = 0.5 + 0.5 * tanh
    return up2, tanh, half


def mlp_forward(hid32, ln_ref, wup_ref, wdown_ref):
    normed, _ = ln_norm(hid32)
    m_in = (normed * ln_ref[2:3, :] + ln_ref[3:4, :]).astype(BF16)
    total = None
    for c in range(4):
        up = dot_nn(m_in, wup_ref[:, c * D:(c + 1) * D])
        act = (up * gelu_parts(up)[2]).astype(BF16)
        part = dot_nn(act, wdown_ref[c * D:(c + 1) * D, :])
        total = part if total is None else total + part
    return (hid32 + total).astype(BF16)


def mlp_backward(hid32, dy, ln_ref, wup_ref, wout_ref, wdown_ref, m_s, act_s, dup_s, dhid_s, datt_s, lng_ref, rows, emit):
    normed, inv_std = ln_norm(hid32)
    m_in = (normed * ln_ref[2:3, :] + ln_ref[3:4, :]).astype(BF16)
    m_s[rows, :] = m_in
    total = None
    dm = None
    for c in range(4):
        cols = slice(c * D, (c + 1) * D)
        up = dot_nn(m_in, wup_ref[:, cols])
        up2, tanh, half = gelu_parts(up)
        act = (up * half).astype(BF16)
        act_s[rows, cols] = act
        if emit is not None:
            part = dot_nn(act, wdown_ref[cols, :])
            total = part if total is None else total + part
        slope = half + (0.5 * up) * (1.0 - tanh * tanh) * (GELU_C + (3.0 * GELU_A * GELU_C) * up2)
        d_act = dot_nt(dy, wdown_ref[cols, :]).astype(BF16).astype(F32)
        d_up = (d_act * slope).astype(BF16)
        dup_s[rows, cols] = d_up
        d_part = dot_nt(d_up, wup_ref[:, cols])
        dm = d_part if dm is None else dm + d_part
    if emit is not None:
        emit[rows, :] = (hid32 + total).astype(BF16)
    dm32 = dm.astype(BF16).astype(F32)
    lng_ref[2:3, :] += jnp.sum(dm32 * normed, axis=0, keepdims=True)
    lng_ref[3:4, :] += jnp.sum(dm32, axis=0, keepdims=True)
    d_hid32 = ln_back(dm32, normed, inv_std, ln_ref[2:3, :])
    d_hid = (d_hid32 + dy.astype(F32)).astype(BF16)
    dhid_s[rows, :] = d_hid
    datt_s[rows, :] = dot_nt(d_hid, wout_ref[...]).astype(BF16)


def mlp_grads(g_ref, m_s, act_s, dup_s, dhid_s, o_s, dy_ref):
    def chunk(c, _):
        cols = pl.ds(pl.multiple_of(c * D, D), D)
        g_ref[4 + c] = dot_tn(m_s[...], dup_s[:, cols])
        g_ref[8 + c] = dot_tn(act_s[:, cols], dy_ref[...])
        return 0
    lax.fori_loop(0, 4, chunk, 0)
    g_ref[3] = dot_tn(o_s[...], dhid_s[...])


def attn_backward(qkv_s, p_s, datt_s, dqkv_s, first=0, last=6):
    def heads(i, rows, pair):
        q2 = qkv_s[rows, pair_cols(0, pair)]
        k2 = qkv_s[rows, pair_cols(1, pair)]
        v2 = qkv_s[rows, pair_cols(2, pair)]
        do2 = datt_s[rows, pair_cols(0, pair)]
        dqs, dks, dvs = [], [], []
        for e in range(2):
            cut = slice(e * 64, e * 64 + 64)
            probs = p_s[i * 2 + e]
            d_out = do2[:, cut]
            d_probs = dot_nt(d_out, v2[:, cut]).astype(BF16).astype(F32)
            p32 = probs.astype(F32)
            row_dot = jnp.sum(d_probs * p32, axis=-1, keepdims=True)
            d_scores = (p32 * (d_probs - row_dot) * 0.125).astype(BF16)
            dqs.append(dot_nn(d_scores, k2[:, cut]).astype(BF16))
            dks.append(dot_tn(d_scores, q2[:, cut]).astype(BF16))
            dvs.append(dot_tn(probs, d_out).astype(BF16))
        dqkv_s[rows, pair_cols(0, pair)] = jnp.concatenate(dqs, axis=1)
        dqkv_s[rows, pair_cols(1, pair)] = jnp.concatenate(dks, axis=1)
        dqkv_s[rows, pair_cols(2, pair)] = jnp.concatenate(dvs, axis=1)
    head_pairs(heads, first, last)


def qkv_backward(x_ref, dqkv_s, dhid_s, ln_ref, wqkv_ref, a_s, dx_ref, lng_ref):
    def tile(rows):
        normed, inv_std = ln_norm(x_ref[rows, :].astype(F32))
        a_s[rows, :] = (normed * ln_ref[0:1, :] + ln_ref[1:2, :]).astype(BF16)
        da32 = dot_nt(dqkv_s[rows, :], wqkv_ref[...]).astype(BF16).astype(F32)
        lng_ref[0:1, :] += jnp.sum(da32 * normed, axis=0, keepdims=True)
        lng_ref[1:2, :] += jnp.sum(da32, axis=0, keepdims=True)
        d_in = ln_back(da32, normed, inv_std, ln_ref[0:1, :])
        dx_ref[rows, :] = (d_in + dhid_s[rows, :].astype(F32)).astype(BF16)
    row_tiles(tile)


def qkv_grads(g_ref, a_s, dqkv_s):
    def chunk(c, _):
        g_ref[c] = dot_tn(a_s[...], dqkv_s[:, pl.ds(pl.multiple_of(c * D, D), D)])
        return 0
    lax.fori_loop(0, 3, chunk, 0)


def to_pieces(act_s, snd_ref):
    for a in range(2):
        snd_ref[:, a] = act_s[a * SEQ:(a + 1) * SEQ, :].reshape(SEQ // 2, 2, D)


def from_pieces(rcv_ref, dst_ref):
    flat = rcv_ref[...].reshape(T, D)
    row = lax.broadcasted_iota(jnp.int32, (SEQ, T), 0)
    col = lax.broadcasted_iota(jnp.int32, (SEQ, T), 1)
    for b in range(2):
        pick = (col == 2 * row + b).astype(F32).astype(BF16)
        dst_ref[b * SEQ:(b + 1) * SEQ, :] = dot_nn(pick, flat).astype(BF16)


HALF = D // 2
SIZES = (96, 48, 24, 24, 24, 24)
RECV_OFF = (0, 96, 144, 168, 192, 216)
RECV_ROWS = 240
HALVINGS = 3
ROUND_BLOCKS = ((4, 5, 6, 7, 8, 9), (10, 11, 3, 0, 1, 2))


def dim_info(me, dim):
    axis, far = dim // 2, dim % 2
    stride = (2, 8, 32)[axis]
    coord = lax.rem(lax.div(me, stride), 4)
    if far:
        bit = lax.div(coord, 2)
        partner = me + (3 - 2 * coord) * stride
    else:
        bit = lax.rem(coord + lax.div(coord, 2), 2)
        partner = me + (1 - 2 * lax.rem(coord, 2)) * stride
    return bit, partner


def remote_copy(src, dst, s_sem, r_sem, to):
    return pltpu.make_async_remote_copy(src, dst, s_sem, r_sem, device_id={"sp": to}, device_id_type=MESH)


def rows_at(start, size):
    return pl.ds(pl.multiple_of(start, 8), size)


class Round:
    def __init__(self, index, grads, blocks, out_refs, me, dims, half, recv, sems):
        self.r = index
        self.g = grads
        self.blocks = blocks
        self.out_refs = out_refs
        self.core = lax.rem(me, 2)
        self.sibling = me + 1 - 2 * self.core
        self.dims = dims
        self.half = half
        self.recv = recv
        (self.half_send, self.half_recv, self.send_sem, self.recv_sem, self.back_send, self.back_recv,
         self.fwd_send, self.fwd_recv, self.out_sem, self.free_sem, self.core_free) = sems
        self.offs = {(p, 0): self.core * HALF for p in range(6)}
        self.copies = {}
        self.forwards = {p: [] for p in range(6)}
        self.outs = []

    def start_core(self, parts=range(6)):
        for p in parts:
            copy = remote_copy(self.g.at[self.blocks[p], rows_at((1 - self.core) * HALF, HALF)], self.half.at[self.r, p],
                               self.half_send.at[self.r, p], self.half_recv.at[self.r, p], self.sibling)
            copy.start()
            self.copies["core", p] = copy

    def join_core(self):
        for p in range(6):
            self.copies["core", p].wait()
            pl.semaphore_signal(self.core_free.at[self.r, p], inc=1, device_id={"sp": self.sibling}, device_id_type=MESH)
            self.g[self.blocks[p], rows_at(self.core * HALF, HALF)] += self.half[self.r, p]
            self.start_send(0, p)

    def start_send(self, t, p):
        bit, partner = self.dims[(p + t) % 6]
        off, size = self.offs[p, t], SIZES[t]
        keep, give = (off + bit * size, off + (1 - bit) * size) if t < HALVINGS else (off, off)
        self.offs[p, t + 1] = keep
        copy = remote_copy(self.g.at[self.blocks[p], rows_at(give, size)], self.recv.at[self.r, p, pl.ds(RECV_OFF[t], size)],
                           self.send_sem.at[self.r, t, p], self.recv_sem.at[self.r, t, p], partner)
        copy.start()
        self.copies["send", t, p] = copy

    def step(self, t):
        size = SIZES[t]
        for p in range(6):
            self.copies["send", t, p].wait()
            if t < HALVINGS:
                pl.semaphore_signal(self.free_sem.at[self.r, t, p], inc=1, device_id={"sp": self.dims[(p + t) % 6][1]},
                                    device_id_type=MESH)
            self.g[self.blocks[p], rows_at(self.offs[p, t + 1], size)] += self.recv[self.r, p, pl.ds(RECV_OFF[t], size)]
            if t < 5:
                self.start_send(t + 1, p)
            else:
                self.start_back(HALVINGS - 1, p)
                pl.semaphore_wait(self.core_free.at[self.r, p], 1)
                self.forward(p, self.offs[p, HALVINGS], SIZES[HALVINGS - 1])

    def start_back(self, t, p):
        pl.semaphore_wait(self.free_sem.at[self.r, t, p], 1)
        rows = self.g.at[self.blocks[p], rows_at(self.offs[p, t + 1], SIZES[t])]
        copy = remote_copy(rows, rows, self.back_send.at[self.r, t, p], self.back_recv.at[self.r, t, p],
                           self.dims[(p + t) % 6][1])
        copy.start()
        self.copies["back", t, p] = copy

    def forward(self, p, off, size):
        rows = self.g.at[self.blocks[p], rows_at(off, size)]
        slot = len(self.forwards[p])
        copy = remote_copy(rows, rows, self.fwd_send.at[self.r, slot, p], self.fwd_recv.at[self.r, slot, p], self.sibling)
        copy.start()
        self.forwards[p].append(copy)

    def back(self, t):
        for p in range(6):
            self.copies["back", t, p].wait()
            if t > 0:
                self.start_back(t - 1, p)
            bit = self.dims[(p + t) % 6][0]
            self.forward(p, self.offs[p, t + 1] + (1 - 2 * bit) * SIZES[t], SIZES[t])

    def write(self):
        for p in range(6):
            for copy in self.forwards[p]:
                copy.wait()
            copy = pltpu.make_async_copy(self.g.at[self.blocks[p]], self.out_refs[self.blocks[p]], self.out_sem.at[self.r, p])
            copy.start()
            self.outs.append(copy)

    def finish(self):
        for copy in self.outs:
            copy.wait()


def out_slices(blk, gqkv, gout, gup, gdown):
    cols = [pl.ds(c * D, D) for c in range(4)]
    return ([gqkv.at[blk, :, cols[c]] for c in range(3)] + [gout.at[blk]] + [gup.at[blk, :, cols[c]] for c in range(4)]
            + [gdown.at[blk, cols[c]] for c in range(4)])


def step_kernel(n, x_hbm, cot_hbm, ln_in, wqkv_hbm, wout_hbm, wup_hbm, wdown_hbm,
                y_ref, dx_ref, gln_ref, gqkv, gout, gup, gdown,
                x_s, cot_s, mid_s, dmid_s, act_a, ln_s, wqkv, wout, wup, wdown, qkv_s, p_s, o_s, h_s,
                m_s, act_s, dup_s, dhid_s, datt_s, dqkv_s, a_s, snd, rcv, grads, half, recv, lnacc, lnrecv,
                load_sem, swap_send, swap_recv, swap_local, *sems):
    me = lax.axis_index("sp")
    dims = [dim_info(me, d) for d in range(6)]
    sibling = me + 1 - 2 * lax.rem(me, 2)
    ln_send, ln_recv = sems[-2:]
    sems = sems[:-2]

    barrier = pltpu.get_barrier_semaphore()

    def greet(k, _):
        pl.semaphore_signal(barrier, inc=1, device_id={"sp": lax.rem(me + k, n)}, device_id_type=MESH)
        return 0
    lax.fori_loop(1, n, greet, 0)

    loads = {}
    for name, src, dst in (("x", x_hbm, x_s), ("qkv0", wqkv_hbm.at[0], wqkv.at[0]), ("cot", cot_hbm, cot_s),
                           ("out0", wout_hbm.at[0], wout.at[0]), ("up0", wup_hbm.at[0], wup.at[0]),
                           ("down0", wdown_hbm.at[0], wdown.at[0]), ("qkv1", wqkv_hbm.at[1], wqkv.at[1]),
                           ("out1", wout_hbm.at[1], wout.at[1]), ("up1", wup_hbm.at[1], wup.at[1]),
                           ("down1", wdown_hbm.at[1], wdown.at[1])):
        loads[name] = pltpu.make_async_copy(src, dst, load_sem.at[len(loads)])
        loads[name].start()

    def need(*names):
        for name in names:
            loads[name].wait()

    def remote_piece(i, k):
        to = lax.rem(me + k, n)
        return remote_copy(snd.at[i, to], rcv.at[i, me], swap_send.at[i], swap_recv.at[i], to)

    def start_swap(i):
        pltpu.make_async_copy(snd.at[i, me], rcv.at[i, me], swap_local.at[i]).start()

        def send(k, _):
            remote_piece(i, k).start()
            return 0
        lax.fori_loop(1, n, send, 0)

    def end_swap(i):
        pltpu.make_async_copy(snd.at[i, me], rcv.at[i, me], swap_local.at[i]).wait()
        rest = pl.ds(0, n - 1)
        pltpu.make_async_copy(snd.at[i, rest], rcv.at[i, rest], swap_send.at[i]).wait()
        pltpu.make_async_copy(snd.at[i, rest], rcv.at[i, rest], swap_recv.at[i]).wait()

    ln_s[...] = ln_in[...].astype(F32)
    lnacc[...] = jnp.zeros_like(lnacc)
    ln = [ln_s.at[i] for i in range(2)]
    lng = [lnacc.at[pl.ds(8 * i, 8)] for i in range(2)]
    saved = [(qkv_s.at[i], p_s.at[i], o_s.at[i]) for i in range(2)]
    rounds = []
    for i in (1, 0):
        slices = out_slices(i, gqkv, gout, gup, gdown)
        for blocks in ROUND_BLOCKS:
            rounds.append(Round(len(rounds), grads.at[i], blocks, slices, me, dims, half, recv, sems))
    r1, r2, r3, r4 = rounds

    need("x", "qkv0")
    attn_forward(x_s, ln[0], wqkv.at[0], *saved[0])
    need("cot")
    to_pieces(cot_s, snd.at[0])
    pl.semaphore_wait(barrier, n - 1)
    start_swap(0)
    need("out0", "up0", "down0")

    def spatial_tail(rows):
        hid32 = hidden(x_s, o_s.at[0], wout.at[0], h_s.at[0], rows)
        mid_s[rows, :] = mlp_forward(hid32, ln[0], wup.at[0], wdown.at[0])
    row_tiles(spatial_tail)
    to_pieces(mid_s, snd.at[1])
    start_swap(1)

    need("qkv1", "out1", "up1", "down1")
    end_swap(0)
    from_pieces(rcv.at[0], cot_s)
    end_swap(1)
    from_pieces(rcv.at[1], mid_s)
    attn_forward(mid_s, ln[1], wqkv.at[1], *saved[1])

    def temporal_tail(rows):
        hid32 = hidden(mid_s, o_s.at[1], wout.at[1], h_s.at[1], rows)
        mlp_backward(hid32, cot_s[rows, :], ln[1], wup.at[1], wout.at[1], wdown.at[1], m_s, act_s, dup_s, dhid_s, datt_s,
                     lng[1], rows, act_a)
    row_tiles(temporal_tail)
    to_pieces(act_a, snd.at[2])
    start_swap(2)
    attn_backward(qkv_s.at[1], p_s.at[1], datt_s, dqkv_s)
    qkv_backward(mid_s, dqkv_s, dhid_s, ln[1], wqkv.at[1], a_s, dmid_s, lng[1])
    to_pieces(dmid_s, snd.at[3])
    start_swap(3)
    mlp_grads(grads.at[1], m_s, act_s, dup_s, dhid_s, o_s.at[1], cot_s)
    r1.start_core()
    qkv_grads(grads.at[1], a_s, dqkv_s)
    r2.start_core()
    end_swap(2)
    from_pieces(rcv.at[2], y_ref)
    r1.join_core()
    r2.join_core()
    end_swap(3)
    from_pieces(rcv.at[3], dmid_s)

    def back_tail(rows):
        mlp_backward(h_s[0, rows, :].astype(F32), dmid_s[rows, :], ln[0], wup.at[0], wout.at[0], wdown.at[0], m_s, act_s,
                     dup_s, dhid_s, datt_s, lng[0], rows, None)
    row_tiles(back_tail, 0, 2)
    r1.step(0)
    r2.step(0)
    row_tiles(back_tail, 2, 4)
    r1.step(1)
    r2.step(1)
    mlp_grads(grads.at[0], m_s, act_s, dup_s, dhid_s, o_s.at[0], dmid_s)
    r3.start_core()
    r1.step(2)
    r2.step(2)
    attn_backward(qkv_s.at[0], p_s.at[0], datt_s, dqkv_s, 0, 3)
    r1.step(3)
    r2.step(3)
    r3.join_core()
    attn_backward(qkv_s.at[0], p_s.at[0], datt_s, dqkv_s, 3, 6)
    r1.step(4)
    r2.step(4)
    r3.step(0)
    qkv_backward(x_s, dqkv_s, dhid_s, ln[0], wqkv.at[0], a_s, dx_ref, lng[0])
    r1.step(5)
    r2.step(5)
    r3.step(1)

    ln_copies = []

    def ln_start(t):
        to = sibling if t == 0 else dims[t - 1][1]
        copy = remote_copy(lnacc, lnrecv.at[t], ln_send.at[t], ln_recv.at[t], to)
        copy.start()
        ln_copies.append(copy)

    def ln_next():
        t = len(ln_copies) - 1
        ln_copies[t].wait()
        lnacc[...] += lnrecv[t]
        if t < 6:
            ln_start(t + 1)

    ln_start(0)
    qkv_grads(grads.at[0], a_s, dqkv_s)
    r4.start_core()
    r1.back(2)
    r2.back(2)
    r3.step(2)
    ln_next()
    r4.join_core()
    r1.back(1)
    r3.step(3)
    ln_next()
    r4.step(0)
    r2.back(1)
    r3.step(4)
    ln_next()
    r4.step(1)
    r1.back(0)
    r3.step(5)
    ln_next()
    r4.step(2)
    r2.back(0)
    r3.back(2)
    ln_next()
    r4.step(3)
    r3.back(1)
    ln_next()
    r4.step(4)
    r3.back(0)
    ln_next()
    r1.write()
    r2.write()
    r4.step(5)
    r4.back(2)
    r4.back(1)
    r3.write()
    r4.back(0)
    for i in range(2):
        gln_ref[i] = lnacc[8 * i:8 * i + 4, :]
    r4.write()
    for rnd in rounds:
        rnd.finish()


def device_step(n, latents, cotangent, ln_params, w_qkv, w_out, w_up, w_down):
    dma = pltpu.SemaphoreType.DMA
    regular = pltpu.SemaphoreType.REGULAR
    any_spec = pl.BlockSpec(memory_space=pl.ANY)
    vmem_spec = pl.BlockSpec(memory_space=pltpu.VMEM)
    act, wide, qkv = (T, D), (T, FF), (T, 3 * D)
    y, dx, gln, gqkv, gout, gup, gdown = pl.pallas_call(
        functools.partial(step_kernel, n),
        out_shape=[jax.ShapeDtypeStruct(act, BF16)] * 2 + [jax.ShapeDtypeStruct(s, F32) for s in (
            (2, 4, D), (2, D, 3 * D), (2, D, D), (2, D, FF), (2, FF, D))],
        in_specs=[any_spec, any_spec, vmem_spec] + [any_spec] * 4,
        out_specs=[vmem_spec] * 3 + [any_spec] * 4,
        scratch_shapes=[pltpu.VMEM(s, BF16) for s in [act] * 5]
        + [pltpu.VMEM((2, 4, D), F32)]
        + [pltpu.VMEM((2,) + s, BF16) for s in ((D, 3 * D), (D, D), (D, FF), (FF, D), qkv, (12, SEQ, SEQ), act, act)]
        + [pltpu.VMEM(s, BF16) for s in (act, wide, wide, act, act, qkv, act)]
        + [pltpu.VMEM((4, n, 2, 2, D), BF16)] * 2
        + [pltpu.VMEM((2, 12, D, D), F32), pltpu.VMEM((4, 6, HALF, D), F32), pltpu.VMEM((4, 6, RECV_ROWS, D), F32),
           pltpu.VMEM((16, D), F32), pltpu.VMEM((7, 16, D), F32)]
        + [dma((10,)), dma((4,)), dma((4,)), dma((4,))]
        + [dma((4, 6)), dma((4, 6)), dma((4, 6, 6)), dma((4, 6, 6)), dma((4, 3, 6)), dma((4, 3, 6)), dma((4, 4, 6)),
           dma((4, 4, 6)), dma((4, 6)), regular((4, 3, 6)), regular((4, 6)), dma((7,)), dma((7,))],
        compiler_params=pltpu.CompilerParams(collective_id=0, has_side_effects=True, vmem_limit_bytes=67_000_000),
        cost_estimate=pl.CostEstimate(flops=12_000_000_000, bytes_accessed=30_000_000, transcendentals=0),
    )(latents.reshape(T, D), cotangent.reshape(T, D), ln_params, w_qkv, w_out.reshape(2, D, D), w_up, w_down)
    return (y.reshape(latents.shape), dx.reshape(latents.shape), gln, gqkv, gout.reshape(2, 6, 64, D), gup, gdown)


def solution(mesh):
    act_spec = P('data', 'sp', None, None)
    replicated = P()
    part_spec = P('data')
    return jax.shard_map(functools.partial(device_step, mesh.shape["sp"]), mesh=mesh,
                         in_specs=(act_spec, act_spec, replicated, replicated, replicated, replicated, replicated),
                         out_specs=(act_spec, act_spec, part_spec, part_spec, part_spec, part_spec, part_spec),
                         check_vma=False)
```

time: 312 us -> 176 us (0.56)
  Pallas kernels: 252 us -> 159 us
  local copies, waits for them, and re-layouts: 48.5 us -> 15.9 us
  other arithmetic: 10.5 us -> 0.01 us
    pallas_call x8 -> x1, Pallas kernels: 252 us -> 159 us  [device_step(): pl.pallas_call(functools.partial(step_kernel, n), out_shape=[jax.ShapeDty...]
    reshape x20 -> x0, local copies, waits for them, and re-layouts: 15.3 us -> none  [the longest x10 8.31 us: from_pieces(): return pieces.reshape(n, 2, 2, D).transpose(2, 0, 1, 3).reshape(T, D)]
    transpose x2 -> x0, local copies, waits for them, and re-layouts: 9.4 us -> none  [wide(): blocks[:, first:first + count].transpose(0, 2, 1, 3)]
    squeeze x4 -> x0, local copies, waits for them, and re-layouts: 6.6 us -> none  [the longest x1 2.8 us: device_step(): w_qkv[i]]
    another operation x2 -> x0, other arithmetic: 6.45 us -> none  [device_step(): blocks = jnp.stack([r0, r1])]
    unnamed x16 -> x17, local copies, waits for them, and re-layouts: 11.3 us -> 15.9 us
    slice x2 -> x0, local copies, waits for them, and re-layouts: 3.6 us -> none  [the longest x1 2.11 us: device_step(): w_out[i].reshape(D, D)]
where the time goes in v2:
time: 176 us
  Pallas kernels  159 us (90%)
  local copies, waits for them, and re-layouts  15.9 us (9%)
    pallas_call x1, Pallas kernels, device_step(): pl.pallas_call(functools.partial(step_kernel, n), out_shape=[jax.ShapeDty...  159 us
    unnamed x17, local copies, waits for them, and re-layouts  15.9 us

profile of v2, /device:TPU:1, one launch (start us, length us, event | category | flops | bytes accessed | tf_op | source)
XLA Modules:
  0.0 175.9 jit_solution(4967872784395426980)
XLA Ops:
  0.6 159.3 %shard_map.126 = (bf16[512,384]{1,0:T(8,128)(2,1)}, bf16[512,384]{1,0:T(8,128)(2,1)}, f32[2,4,384]{2,1,0:T(4,128)}, f32[2,384,1152]{2,1,0:T(8,128)}, f32[2,384,3...) custom-call(bf16[512,384]{1,0:T(8,128)(2,1)} %bitcast.14, bf16[512,384]{1,0:T(8,128)(2,1)} %bitcast.15, ...), custom_call_target="tpu_custom_call" | custom-call | flops 12000000000 | bytes 30000000 | tf_op jit(solution)/shard_map/pallas_call | solution.py:541
  159.9 1.8 %copy.21 = bf16[1,2,256,384]{3,2,1,0:T(8,128)(2,1)} copy(bf16[1,2,256,384]{3,2,1,0:T(8,128)(2,1)} %bitcast.12) | data formatting | bytes 786432
  161.7 1.8 %copy.22 = bf16[1,2,256,384]{3,2,1,0:T(8,128)(2,1)} copy(bf16[1,2,256,384]{3,2,1,0:T(8,128)(2,1)} %bitcast.11) | data formatting | bytes 786432
  163.5 0.0 slice-start.2
  163.5 1.5 copy.23
  164.9 0.0 copy-start
  164.9 0.0 slice-start.3
  164.9 4.1 %copy.24 = f32[2,384,1152]{2,1,0:T(8,128)} copy(f32[2,384,1152]{2,1,0:T(8,128)} %get-tuple-element.31) | data formatting | bytes 7077888
  169.1 0.0 copy-done
  169.1 0.0 slice-start
  169.1 1.0 copy.25
  170.1 0.0 slice-done.2
  170.1 0.0 slice-done.3
  170.1 0.0 slice-start.1
  170.1 2.4 %copy.26 = f32[2,384,1536]{2,1,0:T(8,128)} copy(f32[2,384,1536]{2,1,0:T(8,128)S(1)} %bitcast.9) | data formatting | bytes 9437184
  172.5 0.8 slice-done
  173.3 0.3 slice-done.1
  173.7 2.2 %copy.27 = f32[2,1536,384]{2,1,0:T(8,128)} copy(f32[2,1536,384]{2,1,0:T(8,128)S(1)} %bitcast.7) | data formatting | bytes 9437184
  (2 shorter events, 0.0 us)
Async XLA Ops:
  163.5 6.6 %slice-start.2 = ((s8[4718592]{0:T(1024)(128)(4,1)}), s8[4194304]{0:T(1024)(128)(4,1)S(1)}, s32[]{:S(2)}) async-start(s8[4718592]{0:T(1024)(128)(4,1)} %bitcast.8), calls=%async_computation.2 | async-start | bytes 8388608
  164.9 4.2 %copy-start = (f32[2,384,384]{2,1,0:T(8,128)S(1)}, f32[2,384,384]{2,1,0:T(8,128)}, u32[]{:S(2)}) copy-start(f32[2,384,384]{2,1,0:T(8,128)} %get-tuple-element.18) | copy-start | bytes 3538948
  164.9 5.2 %slice-start.3 = ((s8[4718592]{0:T(1024)(128)(4,1)}), s8[524288]{0:T(1024)(128)(4,1)S(1)}, s32[]{:S(2)}) async-start(s8[4718592]{0:T(1024)(128)(4,1)} %bitcast.8), calls=%async_computation.3 | async-start | bytes 1048576
  169.1 4.2 %slice-start = ((s8[4718592]{0:T(1024)(128)(4,1)}), s8[4194304]{0:T(1024)(128)(4,1)S(1)}, s32[]{:S(2)}) async-start(s8[4718592]{0:T(1024)(128)(4,1)} %bitcast.6), calls=%async_computation | async-start | bytes 8388608
  170.1 3.5 %slice-start.1 = ((s8[4718592]{0:T(1024)(128)(4,1)}), s8[524288]{0:T(1024)(128)(4,1)S(1)}, s32[]{:S(2)}) async-start(s8[4718592]{0:T(1024)(128)(4,1)} %bitcast.6), calls=%async_computation.1 | async-start | bytes 1048576

commit v3 on v2

--- a/solution.py
+++ b/solution.py
@@ -15,7 +15,7 @@
 FF = 1536
 ROWS = 128
 MESH = pl.DeviceIdType.MESH
-VMEM_LIMIT = 60 * 1024 * 1024
+STEP_VMEM = 48_000_000
 GELU_C = 0.7978845608028654
 GELU_A = 0.044715
 
@@ -245,22 +245,20 @@
 
 
 class Round:
-    def __init__(self, index, grads, blocks, out_refs, me, dims, half, recv, sems):
+    def __init__(self, index, grads, blocks, me, dims, half, recv, sems):
         self.r = index
         self.g = grads
         self.blocks = blocks
-        self.out_refs = out_refs
         self.core = lax.rem(me, 2)
         self.sibling = me + 1 - 2 * self.core
         self.dims = dims
         self.half = half
         self.recv = recv
         (self.half_send, self.half_recv, self.send_sem, self.recv_sem, self.back_send, self.back_recv,
-         self.fwd_send, self.fwd_recv, self.out_sem, self.free_sem, self.core_free) = sems
+         self.fwd_send, self.fwd_recv, self.free_sem, self.core_free) = sems
         self.offs = {(p, 0): self.core * HALF for p in range(6)}
         self.copies = {}
         self.forwards = {p: [] for p in range(6)}
-        self.outs = []
 
     def start_core(self, parts=range(6)):
         for p in parts:
@@ -324,17 +322,10 @@
             bit = self.dims[(p + t) % 6][0]
             self.forward(p, self.offs[p, t + 1] + (1 - 2 * bit) * SIZES[t], SIZES[t])
 
-    def write(self):
+    def finish(self):
         for p in range(6):
             for copy in self.forwards[p]:
                 copy.wait()
-            copy = pltpu.make_async_copy(self.g.at[self.blocks[p]], self.out_refs[self.blocks[p]], self.out_sem.at[self.r, p])
-            copy.start()
-            self.outs.append(copy)
-
-    def finish(self):
-        for copy in self.outs:
-            copy.wait()
 
 
 def out_slices(blk, gqkv, gout, gup, gdown):
@@ -344,9 +335,9 @@
 
 
 def step_kernel(n, x_hbm, cot_hbm, ln_in, wqkv_hbm, wout_hbm, wup_hbm, wdown_hbm,
-                y_ref, dx_ref, gln_ref, gqkv, gout, gup, gdown,
+                y_ref, dx_ref, gln_ref, grads,
                 x_s, cot_s, mid_s, dmid_s, act_a, ln_s, wqkv, wout, wup, wdown, qkv_s, p_s, o_s, h_s,
-                m_s, act_s, dup_s, dhid_s, datt_s, dqkv_s, a_s, snd, rcv, grads, half, recv, lnacc, lnrecv,
+                m_s, act_s, dup_s, dhid_s, datt_s, dqkv_s, a_s, snd, rcv, half, recv, lnacc, lnrecv,
                 load_sem, swap_send, swap_recv, swap_local, *sems):
     me = lax.axis_index("sp")
     dims = [dim_info(me, d) for d in range(6)]
@@ -399,17 +390,14 @@
     saved = [(qkv_s.at[i], p_s.at[i], o_s.at[i]) for i in range(2)]
     rounds = []
     for i in (1, 0):
-        slices = out_slices(i, gqkv, gout, gup, gdown)
         for blocks in ROUND_BLOCKS:
-            rounds.append(Round(len(rounds), grads.at[i], blocks, slices, me, dims, half, recv, sems))
+            rounds.append(Round(len(rounds), grads.at[i], blocks, me, dims, half, recv, sems))
     r1, r2, r3, r4 = rounds
 
     need("x", "qkv0")
     attn_forward(x_s, ln[0], wqkv.at[0], *saved[0])
     need("cot")
     to_pieces(cot_s, snd.at[0])
-    pl.semaphore_wait(barrier, n - 1)
-    start_swap(0)
     need("out0", "up0", "down0")
 
     def spatial_tail(rows):
@@ -417,14 +405,16 @@
         mid_s[rows, :] = mlp_forward(hid32, ln[0], wup.at[0], wdown.at[0])
     row_tiles(spatial_tail)
     to_pieces(mid_s, snd.at[1])
+    pl.semaphore_wait(barrier, n - 1)
     start_swap(1)
+    start_swap(0)
 
     need("qkv1", "out1", "up1", "down1")
-    end_swap(0)
-    from_pieces(rcv.at[0], cot_s)
     end_swap(1)
     from_pieces(rcv.at[1], mid_s)
     attn_forward(mid_s, ln[1], wqkv.at[1], *saved[1])
+    end_swap(0)
+    from_pieces(rcv.at[0], cot_s)
 
     def temporal_tail(rows):
         hid32 = hidden(mid_s, o_s.at[1], wout.at[1], h_s.at[1], rows)
@@ -518,18 +508,26 @@
     r4.step(4)
     r3.back(0)
     ln_next()
-    r1.write()
-    r2.write()
     r4.step(5)
     r4.back(2)
     r4.back(1)
-    r3.write()
     r4.back(0)
     for i in range(2):
         gln_ref[i] = lnacc[8 * i:8 * i + 4, :]
-    r4.write()
     for rnd in rounds:
         rnd.finish()
+
+
+def publish_kernel(y_in, dx_in, gln_in, grads, y_ref, dx_ref, gln_ref, gqkv, gout, gup, gdown, sem):
+    pairs = [(y_in, y_ref), (dx_in, dx_ref), (gln_in, gln_ref)]
+    for i in range(2):
+        slices = out_slices(i, gqkv, gout, gup, gdown)
+        pairs += [(grads.at[i, j], slices[j]) for j in range(12)]
+    copies = [pltpu.make_async_copy(src, dst, sem.at[k]) for k, (src, dst) in enumerate(pairs)]
+    for copy in copies:
+        copy.start()
+    for copy in copies:
+        copy.wait()
 
 
 def device_step(n, latents, cotangent, ln_params, w_qkv, w_out, w_up, w_down):
@@ -538,25 +536,34 @@
     any_spec = pl.BlockSpec(memory_space=pl.ANY)
     vmem_spec = pl.BlockSpec(memory_space=pltpu.VMEM)
     act, wide, qkv = (T, D), (T, FF), (T, 3 * D)
-    y, dx, gln, gqkv, gout, gup, gdown = pl.pallas_call(
+    shapes = [(act, BF16), (act, BF16), ((2, 4, D), F32)]
+    held = pl.pallas_call(
         functools.partial(step_kernel, n),
-        out_shape=[jax.ShapeDtypeStruct(act, BF16)] * 2 + [jax.ShapeDtypeStruct(s, F32) for s in (
-            (2, 4, D), (2, D, 3 * D), (2, D, D), (2, D, FF), (2, FF, D))],
+        out_shape=[pltpu.VMEM(s, t) for s, t in shapes] + [pltpu.VMEM((2, 12, D, D), F32)],
         in_specs=[any_spec, any_spec, vmem_spec] + [any_spec] * 4,
-        out_specs=[vmem_spec] * 3 + [any_spec] * 4,
+        out_specs=[vmem_spec] * 4,
         scratch_shapes=[pltpu.VMEM(s, BF16) for s in [act] * 5]
         + [pltpu.VMEM((2, 4, D), F32)]
         + [pltpu.VMEM((2,) + s, BF16) for s in ((D, 3 * D), (D, D), (D, FF), (FF, D), qkv, (12, SEQ, SEQ), act, act)]
         + [pltpu.VMEM(s, BF16) for s in (act, wide, wide, act, act, qkv, act)]
         + [pltpu.VMEM((4, n, 2, 2, D), BF16)] * 2
-        + [pltpu.VMEM((2, 12, D, D), F32), pltpu.VMEM((4, 6, HALF, D), F32), pltpu.VMEM((4, 6, RECV_ROWS, D), F32),
+        + [pltpu.VMEM((4, 6, HALF, D), F32), pltpu.VMEM((4, 6, RECV_ROWS, D), F32),
            pltpu.VMEM((16, D), F32), pltpu.VMEM((7, 16, D), F32)]
         + [dma((10,)), dma((4,)), dma((4,)), dma((4,))]
         + [dma((4, 6)), dma((4, 6)), dma((4, 6, 6)), dma((4, 6, 6)), dma((4, 3, 6)), dma((4, 3, 6)), dma((4, 4, 6)),
-           dma((4, 4, 6)), dma((4, 6)), regular((4, 3, 6)), regular((4, 6)), dma((7,)), dma((7,))],
-        compiler_params=pltpu.CompilerParams(collective_id=0, has_side_effects=True, vmem_limit_bytes=67_000_000),
+           dma((4, 4, 6)), regular((4, 3, 6)), regular((4, 6)), dma((7,)), dma((7,))],
+        compiler_params=pltpu.CompilerParams(collective_id=0, has_side_effects=True, vmem_limit_bytes=STEP_VMEM),
         cost_estimate=pl.CostEstimate(flops=12_000_000_000, bytes_accessed=30_000_000, transcendentals=0),
     )(latents.reshape(T, D), cotangent.reshape(T, D), ln_params, w_qkv, w_out.reshape(2, D, D), w_up, w_down)
+    y, dx, gln, gqkv, gout, gup, gdown = pl.pallas_call(
+        publish_kernel,
+        out_shape=[jax.ShapeDtypeStruct(s, t) for s, t in shapes]
+        + [jax.ShapeDtypeStruct(s, F32) for s in ((2, D, 3 * D), (2, D, D), (2, D, FF), (2, FF, D))],
+        in_specs=[vmem_spec] * 4,
+        out_specs=[any_spec] * 7,
+        scratch_shapes=[dma((27,))],
+        compiler_params=pltpu.CompilerParams(vmem_limit_bytes=2_000_000),
+    )(*held)
     return (y.reshape(latents.shape), dx.reshape(latents.shape), gln, gqkv, gout.reshape(2, 6, 64, D), gup, gdown)
 
 

time: 176 us -> 164 us (0.932)
  local copies, waits for them, and re-layouts: 15.9 us -> 0 us
  Pallas kernels: 159 us -> 163 us
    unnamed x17 -> x0, local copies, waits for them, and re-layouts: 15.9 us -> none
    pallas_call x1 -> x2, Pallas kernels: 159 us -> 163 us  [the longest x1 157 us: device_step(): pl.pallas_call(functools.partial(step_kernel, n), out_shape=[pltpu.VMEM(s...]
where the time goes in v3:
time: 164 us; the launch traced here: 163 us
  Pallas kernels  163 us (99%)
    pallas_call x1, Pallas kernels, device_step(): pl.pallas_call(functools.partial(step_kernel, n), out_shape=[pltpu.VMEM(s...  157 us
    pallas_call x1, Pallas kernels, device_step(): pl.pallas_call(publish_kernel, out_shape=[jax.ShapeDtypeStruct(s, t) for...  5.5 us

profile of v3, /device:TPU:1, one launch (start us, length us, event | category | flops | bytes accessed | tf_op | source)
XLA Modules:
  0.0 163.4 jit_solution(1791102365869535036)
XLA Ops:
  0.6 157.1 %shard_map.126 = (bf16[512,384]{1,0:T(8,128)(2,1)S(1)}, bf16[512,384]{1,0:T(8,128)(2,1)S(1)}, f32[2,4,384]{2,1,0:T(4,128)S(1)}, f32[2,12,384,384]{3,2,1,0:T(8,128)S(1)}) custom-call(bf16[512,384]{1,0:T(8,128)(2,1)} %bitcast.8, bf16[512,384]{1,0:T(8,128)(2,1)} %bitcast.9, bf16[2,4,384]{2,1,0:T(4,128)(2,1)} %ln_in.1, bf16[2,384,1152]{2,1,0:T(8,128)(2,1)} %wqkv_hbm.1, ...), custom_call_target="tpu_custom_call" | custom-call | flops 12000000000 | bytes 30000000 | tf_op jit(solution)/shard_map/pallas_call | solution.py:540
  157.7 5.5 %shard_map.127 = (bf16[512,384]{1,0:T(8,128)(2,1)}, bf16[512,384]{1,0:T(8,128)(2,1)}, f32[2,4,384]{2,1,0:T(4,128)}, f32[2,384,1152]{2,1,0:T(8,128)}, f32[2,384,3...) custom-call(bf16[512,384]{1,0:T(8,128)(2,1)S(1)} %get-tuple-element.18.y_in, ...), custom_call_target="tpu_custom_call" | custom-call | tf_op jit(solution)/shard_map/pallas_call | solution.py:558

commit v4 on v3

--- a/solution.py
+++ b/solution.py
@@ -32,11 +32,18 @@
     return lax.dot_general(a, b, (((0,), (0,)), ((), ())), preferred_element_type=F32)
 
 
-def row_tiles(body, first=0, last=T // ROWS):
+def run_events(i, events):
+    for k, event in enumerate(events):
+        if event is not None:
+            pl.when(i == k)(event)
+
+
+def row_tiles(body, events=()):
     def step(i, _):
         body(pl.ds(pl.multiple_of(i * ROWS, ROWS), ROWS))
+        run_events(i, events)
         return 0
-    lax.fori_loop(first, last, step, 0)
+    lax.fori_loop(0, T // ROWS, step, 0)
 
 
 def ln_norm(x32):
@@ -52,14 +59,15 @@
     return inv_std * (d_center - normed * (jnp.sum(d_norm * normed, axis=-1, keepdims=True) * (1.0 / D)))
 
 
-def head_pairs(body, first=0, last=6):
+def head_pairs(body, events=()):
     def step(i, _):
         seq = i // 3
         pair = i - seq * 3
         rows = pl.ds(pl.multiple_of(seq * SEQ, SEQ), SEQ)
         body(i, rows, pair)
+        run_events(i, events)
         return 0
-    lax.fori_loop(first, last, step, 0)
+    lax.fori_loop(0, 6, step, 0)
 
 
 def pair_cols(which, pair):
@@ -148,17 +156,35 @@
     datt_s[rows, :] = dot_nt(d_hid, wout_ref[...]).astype(BF16)
 
 
-def mlp_grads(g_ref, m_s, act_s, dup_s, dhid_s, o_s, dy_ref):
-    def chunk(c, _):
-        cols = pl.ds(pl.multiple_of(c * D, D), D)
-        g_ref[4 + c] = dot_tn(m_s[...], dup_s[:, cols])
-        g_ref[8 + c] = dot_tn(act_s[:, cols], dy_ref[...])
+def up_grad(g_ref, m_s, dup_s, c):
+    g_ref[4 + c] = dot_tn(m_s[...], dup_s[:, pl.ds(pl.multiple_of(c * D, D), D)])
+
+
+def down_grad(g_ref, act_s, dy_ref, c):
+    g_ref[8 + c] = dot_tn(act_s[:, pl.ds(pl.multiple_of(c * D, D), D)], dy_ref[...])
+
+
+def mlp_grads_first(g_ref, m_s, act_s, dup_s, dy_ref):
+    def up(c, _):
+        up_grad(g_ref, m_s, dup_s, c)
         return 0
-    lax.fori_loop(0, 4, chunk, 0)
+    lax.fori_loop(0, 4, up, 0)
+
+    def down(c, _):
+        down_grad(g_ref, act_s, dy_ref, c)
+        return 0
+    lax.fori_loop(0, 2, down, 0)
+
+
+def mlp_grads_last(g_ref, act_s, dhid_s, o_s, dy_ref):
+    def down(c, _):
+        down_grad(g_ref, act_s, dy_ref, c)
+        return 0
+    lax.fori_loop(2, 4, down, 0)
     g_ref[3] = dot_tn(o_s[...], dhid_s[...])
 
 
-def attn_backward(qkv_s, p_s, datt_s, dqkv_s, first=0, last=6):
+def attn_backward(qkv_s, p_s, datt_s, dqkv_s, events=()):
     def heads(i, rows, pair):
         q2 = qkv_s[rows, pair_cols(0, pair)]
         k2 = qkv_s[rows, pair_cols(1, pair)]
@@ -179,7 +205,7 @@
         dqkv_s[rows, pair_cols(0, pair)] = jnp.concatenate(dqs, axis=1)
         dqkv_s[rows, pair_cols(1, pair)] = jnp.concatenate(dks, axis=1)
         dqkv_s[rows, pair_cols(2, pair)] = jnp.concatenate(dvs, axis=1)
-    head_pairs(heads, first, last)
+    head_pairs(heads, events)
 
 
 def qkv_backward(x_ref, dqkv_s, dhid_s, ln_ref, wqkv_ref, a_s, dx_ref, lng_ref):
@@ -215,12 +241,18 @@
         dst_ref[b * SEQ:(b + 1) * SEQ, :] = dot_nn(pick, flat).astype(BF16)
 
 
-HALF = D // 2
-SIZES = (96, 48, 24, 24, 24, 24)
-RECV_OFF = (0, 96, 144, 168, 192, 216)
-RECV_ROWS = 240
-HALVINGS = 3
-ROUND_BLOCKS = ((4, 5, 6, 7, 8, 9), (10, 11, 3, 0, 1, 2))
+EXCHANGE = 24
+ROUND_BLOCKS = ((4, 5, 6, 7, 8, 9), (10, 11, 3, 0, 1, 2), (4, 5, 6, 7, 8, 9), (10, 11, 3), (0, 1, 2))
+ROUND_SIDE = (1, 1, 0, 0, 0)
+
+
+def round_sizes(blocks):
+    keep = rows = D * len(blocks) // 12
+    sizes = []
+    while rows > EXCHANGE:
+        rows //= 2
+        sizes.append(rows)
+    return keep, len(sizes), sizes + [EXCHANGE] * (6 - len(sizes))
 
 
 def dim_info(me, dim):
@@ -245,87 +277,104 @@
 
 
 class Round:
-    def __init__(self, index, grads, blocks, me, dims, half, recv, sems):
+    def __init__(self, index, grads, me, dims, half, recv, sems):
         self.r = index
-        self.g = grads
-        self.blocks = blocks
-        self.core = lax.rem(me, 2)
-        self.sibling = me + 1 - 2 * self.core
+        self.g = grads.at[ROUND_SIDE[index]]
+        self.keep, self.halvings, self.sizes = round_sizes(ROUND_BLOCKS[index])
         self.dims = dims
         self.half = half
         self.recv = recv
+        core = lax.rem(me, 2)
+        self.sibling = me + 1 - 2 * core
         (self.half_send, self.half_recv, self.send_sem, self.recv_sem, self.back_send, self.back_recv,
          self.fwd_send, self.fwd_recv, self.free_sem, self.core_free) = sems
-        self.offs = {(p, 0): self.core * HALF for p in range(6)}
-        self.copies = {}
-        self.forwards = {p: [] for p in range(6)}
-
-    def start_core(self, parts=range(6)):
-        for p in parts:
-            copy = remote_copy(self.g.at[self.blocks[p], rows_at((1 - self.core) * HALF, HALF)], self.half.at[self.r, p],
-                               self.half_send.at[self.r, p], self.half_recv.at[self.r, p], self.sibling)
-            copy.start()
-            self.copies["core", p] = copy
+        per_block = 6 // len(ROUND_BLOCKS[index])
+        self.block = [ROUND_BLOCKS[index][p // per_block] for p in range(6)]
+        first = [2 * self.keep * (p % per_block) for p in range(6)]
+        self.away = [first[p] + (1 - core) * self.keep for p in range(6)]
+        self.offs = {(p, 0): first[p] + core * self.keep for p in range(6)}
+        self.give = {}
+        for p in range(6):
+            for t in range(6):
+                off, size, bit = self.offs[p, t], self.sizes[t], dims[(p + t) % 6][0]
+                halve = t < self.halvings
+                self.offs[p, t + 1] = off + bit * size if halve else off
+                self.give[p, t] = off + (1 - bit) * size if halve else off
+
+    def rows(self, p, off, size):
+        return self.g.at[self.block[p], rows_at(off, size)]
+
+    def partner(self, t, p):
+        return self.dims[(p + t) % 6][1]
+
+    def core_copy(self, p):
+        return remote_copy(self.rows(p, self.away[p], self.keep), self.half.at[p], self.half_send.at[self.r],
+                           self.half_recv.at[self.r], self.sibling)
+
+    def recv_rows(self, t):
+        return pl.ds(sum(self.sizes[:t]), self.sizes[t])
+
+    def send_copy(self, t, p):
+        return remote_copy(self.rows(p, self.give[p, t], self.sizes[t]), self.recv.at[p, self.recv_rows(t)],
+                           self.send_sem.at[self.r], self.recv_sem.at[self.r, t], self.partner(t, p))
+
+    def back_copy(self, t, p):
+        rows = self.rows(p, self.offs[p, t + 1], self.sizes[t])
+        return remote_copy(rows, rows, self.back_send.at[self.r], self.back_recv.at[self.r, t], self.partner(t, p))
+
+    def forward_copy(self, slot, p):
+        last = self.halvings
+        if slot == 0:
+            rows = self.rows(p, self.offs[p, last], self.sizes[last - 1])
+        else:
+            rows = self.rows(p, self.give[p, last - slot], self.sizes[last - slot])
+        return remote_copy(rows, rows, self.fwd_send.at[self.r], self.fwd_recv.at[self.r], self.sibling)
+
+    def wait_bytes(self, ref, *semaphores):
+        for sem in semaphores:
+            pltpu.make_async_copy(ref, ref, sem).wait()
+
+    def start_core(self):
+        for p in range(6):
+            self.core_copy(p).start()
 
     def join_core(self):
+        self.wait_bytes(self.half, self.half_send.at[self.r], self.half_recv.at[self.r])
+        pl.semaphore_signal(self.core_free.at[self.r], inc=1, device_id={"sp": self.sibling}, device_id_type=MESH)
         for p in range(6):
-            self.copies["core", p].wait()
-            pl.semaphore_signal(self.core_free.at[self.r, p], inc=1, device_id={"sp": self.sibling}, device_id_type=MESH)
-            self.g[self.blocks[p], rows_at(self.core * HALF, HALF)] += self.half[self.r, p]
-            self.start_send(0, p)
-
-    def start_send(self, t, p):
-        bit, partner = self.dims[(p + t) % 6]
-        off, size = self.offs[p, t], SIZES[t]
-        keep, give = (off + bit * size, off + (1 - bit) * size) if t < HALVINGS else (off, off)
-        self.offs[p, t + 1] = keep
-        copy = remote_copy(self.g.at[self.blocks[p], rows_at(give, size)], self.recv.at[self.r, p, pl.ds(RECV_OFF[t], size)],
-                           self.send_sem.at[self.r, t, p], self.recv_sem.at[self.r, t, p], partner)
-        copy.start()
-        self.copies["send", t, p] = copy
+            self.g[self.block[p], rows_at(self.offs[p, 0], self.keep)] += self.half[p]
+            self.send_copy(0, p).start()
+
+    def start_back(self, t):
+        pl.semaphore_wait(self.free_sem.at[self.r, t], 6)
+        for p in range(6):
+            self.back_copy(t, p).start()
 
     def step(self, t):
-        size = SIZES[t]
+        size = self.sizes[t]
+        self.wait_bytes(self.recv.at[:, self.recv_rows(t)], self.send_sem.at[self.r], self.recv_sem.at[self.r, t])
         for p in range(6):
-            self.copies["send", t, p].wait()
-            if t < HALVINGS:
-                pl.semaphore_signal(self.free_sem.at[self.r, t, p], inc=1, device_id={"sp": self.dims[(p + t) % 6][1]},
+            if t < self.halvings:
+                pl.semaphore_signal(self.free_sem.at[self.r, t], inc=1, device_id={"sp": self.partner(t, p)},
                                     device_id_type=MESH)
-            self.g[self.blocks[p], rows_at(self.offs[p, t + 1], size)] += self.recv[self.r, p, pl.ds(RECV_OFF[t], size)]
+            self.g[self.block[p], rows_at(self.offs[p, t + 1], size)] += self.recv[p, self.recv_rows(t)]
             if t < 5:
-                self.start_send(t + 1, p)
-            else:
-                self.start_back(HALVINGS - 1, p)
-                pl.semaphore_wait(self.core_free.at[self.r, p], 1)
-                self.forward(p, self.offs[p, HALVINGS], SIZES[HALVINGS - 1])
-
-    def start_back(self, t, p):
-        pl.semaphore_wait(self.free_sem.at[self.r, t, p], 1)
-        rows = self.g.at[self.blocks[p], rows_at(self.offs[p, t + 1], SIZES[t])]
-        copy = remote_copy(rows, rows, self.back_send.at[self.r, t, p], self.back_recv.at[self.r, t, p],
-                           self.dims[(p + t) % 6][1])
-        copy.start()
-        self.copies["back", t, p] = copy
-
-    def forward(self, p, off, size):
-        rows = self.g.at[self.blocks[p], rows_at(off, size)]
-        slot = len(self.forwards[p])
-        copy = remote_copy(rows, rows, self.fwd_send.at[self.r, slot, p], self.fwd_recv.at[self.r, slot, p], self.sibling)
-        copy.start()
-        self.forwards[p].append(copy)
+                self.send_copy(t + 1, p).start()
+        if t == 5:
+            self.start_back(self.halvings - 1)
+            pl.semaphore_wait(self.core_free.at[self.r], 1)
+            for p in range(6):
+                self.forward_copy(0, p).start()
 
     def back(self, t):
+        self.wait_bytes(self.recv.at[:, self.recv_rows(t)], self.back_send.at[self.r], self.back_recv.at[self.r, t])
+        if t > 0:
+            self.start_back(t - 1)
         for p in range(6):
-            self.copies["back", t, p].wait()
-            if t > 0:
-                self.start_back(t - 1, p)
-            bit = self.dims[(p + t) % 6][0]
-            self.forward(p, self.offs[p, t + 1] + (1 - 2 * bit) * SIZES[t], SIZES[t])
+            self.forward_copy(self.halvings - t, p).start()
 
     def finish(self):
-        for p in range(6):
-            for copy in self.forwards[p]:
-                copy.wait()
+        self.wait_bytes(self.half, self.fwd_send.at[self.r], self.fwd_recv.at[self.r])
 
 
 def out_slices(blk, gqkv, gout, gup, gdown):
@@ -337,8 +386,9 @@
 def step_kernel(n, x_hbm, cot_hbm, ln_in, wqkv_hbm, wout_hbm, wup_hbm, wdown_hbm,
                 y_ref, dx_ref, gln_ref, grads,
                 x_s, cot_s, mid_s, dmid_s, act_a, ln_s, wqkv, wout, wup, wdown, qkv_s, p_s, o_s, h_s,
-                m_s, act_s, dup_s, dhid_s, datt_s, dqkv_s, a_s, snd, rcv, half, recv, lnacc, lnrecv,
-                load_sem, swap_send, swap_recv, swap_local, *sems):
+                m_s, act_s, dup_s, dhid_s, datt_s, dqkv_s, a_s, snd, rcv, lnacc, lnrecv, *rest):
+    halves, recvs = rest[:5], rest[5:10]
+    (load_sem, swap_send, swap_recv, swap_local, *sems) = rest[10:]
     me = lax.axis_index("sp")
     dims = [dim_info(me, d) for d in range(6)]
     sibling = me + 1 - 2 * lax.rem(me, 2)
@@ -388,11 +438,8 @@
     ln = [ln_s.at[i] for i in range(2)]
     lng = [lnacc.at[pl.ds(8 * i, 8)] for i in range(2)]
     saved = [(qkv_s.at[i], p_s.at[i], o_s.at[i]) for i in range(2)]
-    rounds = []
-    for i in (1, 0):
-        for blocks in ROUND_BLOCKS:
-            rounds.append(Round(len(rounds), grads.at[i], blocks, me, dims, half, recv, sems))
-    r1, r2, r3, r4 = rounds
+    rounds = [Round(r, grads, me, dims, halves[r], recvs[r], sems) for r in range(5)]
+    r1, r2, r3, r4, r5 = rounds
 
     need("x", "qkv0")
     attn_forward(x_s, ln[0], wqkv.at[0], *saved[0])
@@ -423,95 +470,96 @@
     row_tiles(temporal_tail)
     to_pieces(act_a, snd.at[2])
     start_swap(2)
-    attn_backward(qkv_s.at[1], p_s.at[1], datt_s, dqkv_s)
+    mlp_grads_first(grads.at[1], m_s, act_s, dup_s, cot_s)
+    r1.start_core()
+    attn_backward(qkv_s.at[1], p_s.at[1], datt_s, dqkv_s, (None, None, r1.join_core))
     qkv_backward(mid_s, dqkv_s, dhid_s, ln[1], wqkv.at[1], a_s, dmid_s, lng[1])
     to_pieces(dmid_s, snd.at[3])
     start_swap(3)
-    mlp_grads(grads.at[1], m_s, act_s, dup_s, dhid_s, o_s.at[1], cot_s)
-    r1.start_core()
+    mlp_grads_last(grads.at[1], act_s, dhid_s, o_s.at[1], cot_s)
     qkv_grads(grads.at[1], a_s, dqkv_s)
     r2.start_core()
+    r1.step(0)
     end_swap(2)
     from_pieces(rcv.at[2], y_ref)
-    r1.join_core()
     r2.join_core()
+    r1.step(1)
     end_swap(3)
     from_pieces(rcv.at[3], dmid_s)
 
     def back_tail(rows):
         mlp_backward(h_s[0, rows, :].astype(F32), dmid_s[rows, :], ln[0], wup.at[0], wout.at[0], wdown.at[0], m_s, act_s,
                      dup_s, dhid_s, datt_s, lng[0], rows, None)
-    row_tiles(back_tail, 0, 2)
-    r1.step(0)
-    r2.step(0)
-    row_tiles(back_tail, 2, 4)
-    r1.step(1)
+
+    def both(*steps):
+        def event():
+            for method, *args in steps:
+                method(*args)
+        return event
+
+    row_tiles(back_tail, (both((r1.step, 2)), None, both((r1.step, 3), (r2.step, 0)), None))
+    mlp_grads_first(grads.at[0], m_s, act_s, dup_s, dmid_s)
+    r3.start_core()
+    r1.step(4)
     r2.step(1)
-    mlp_grads(grads.at[0], m_s, act_s, dup_s, dhid_s, o_s.at[0], dmid_s)
-    r3.start_core()
-    r1.step(2)
-    r2.step(2)
-    attn_backward(qkv_s.at[0], p_s.at[0], datt_s, dqkv_s, 0, 3)
-    r1.step(3)
-    r2.step(3)
-    r3.join_core()
-    attn_backward(qkv_s.at[0], p_s.at[0], datt_s, dqkv_s, 3, 6)
-    r1.step(4)
-    r2.step(4)
-    r3.step(0)
+    mlp_grads_last(grads.at[0], act_s, dhid_s, o_s.at[0], dmid_s)
+    r4.start_core()
+    attn_backward(qkv_s.at[0], p_s.at[0], datt_s, dqkv_s, (
+        both((r3.join_core,), (r1.step, 5)), both((r2.step, 2),), both((r4.join_core,)), both((r1.back, 2)),
+        both((r2.step, 3)), both((r3.step, 0))))
     qkv_backward(x_s, dqkv_s, dhid_s, ln[0], wqkv.at[0], a_s, dx_ref, lng[0])
-    r1.step(5)
-    r2.step(5)
-    r3.step(1)
-
-    ln_copies = []
-
-    def ln_start(t):
+    def ln_copy(t):
         to = sibling if t == 0 else dims[t - 1][1]
-        copy = remote_copy(lnacc, lnrecv.at[t], ln_send.at[t], ln_recv.at[t], to)
-        copy.start()
-        ln_copies.append(copy)
-
-    def ln_next():
-        t = len(ln_copies) - 1
-        ln_copies[t].wait()
+        return remote_copy(lnacc, lnrecv.at[t], ln_send.at[0], ln_recv.at[t], to)
+
+    def ln_next(t):
+        ln_copy(t).wait()
         lnacc[...] += lnrecv[t]
         if t < 6:
-            ln_start(t + 1)
-
-    ln_start(0)
+            ln_copy(t + 1).start()
+
+    ln_copy(0).start()
     qkv_grads(grads.at[0], a_s, dqkv_s)
-    r4.start_core()
-    r1.back(2)
+    r5.start_core()
+    r2.step(4)
+    r4.step(0)
+    r1.back(1)
+    r3.step(1)
+    ln_next(0)
+    r5.join_core()
+    r2.step(5)
+    r4.step(1)
+    r3.step(2)
+    r1.back(0)
+    r5.step(0)
+    ln_next(1)
     r2.back(2)
-    r3.step(2)
-    ln_next()
-    r4.join_core()
-    r1.back(1)
     r3.step(3)
-    ln_next()
-    r4.step(0)
+    r4.step(2)
+    r5.step(1)
+    ln_next(2)
     r2.back(1)
     r3.step(4)
-    ln_next()
-    r4.step(1)
-    r1.back(0)
+    r4.step(3)
+    r5.step(2)
+    ln_next(3)
     r3.step(5)
-    ln_next()
-    r4.step(2)
+    r4.step(4)
+    r5.step(3)
+    ln_next(4)
     r2.back(0)
     r3.back(2)
-    ln_next()
-    r4.step(3)
+    r4.step(5)
+    r5.step(4)
+    ln_next(5)
     r3.back(1)
-    ln_next()
-    r4.step(4)
+    r4.back(1)
+    r5.step(5)
+    ln_next(6)
+    r5.back(1)
     r3.back(0)
-    ln_next()
-    r4.step(5)
-    r4.back(2)
-    r4.back(1)
     r4.back(0)
+    r5.back(0)
     for i in range(2):
         gln_ref[i] = lnacc[8 * i:8 * i + 4, :]
     for rnd in rounds:
@@ -547,11 +595,12 @@
         + [pltpu.VMEM((2,) + s, BF16) for s in ((D, 3 * D), (D, D), (D, FF), (FF, D), qkv, (12, SEQ, SEQ), act, act)]
         + [pltpu.VMEM(s, BF16) for s in (act, wide, wide, act, act, qkv, act)]
         + [pltpu.VMEM((4, n, 2, 2, D), BF16)] * 2
-        + [pltpu.VMEM((4, 6, HALF, D), F32), pltpu.VMEM((4, 6, RECV_ROWS, D), F32),
-           pltpu.VMEM((16, D), F32), pltpu.VMEM((7, 16, D), F32)]
+        + [pltpu.VMEM((16, D), F32), pltpu.VMEM((7, 16, D), F32)]
+        + [pltpu.VMEM((6, round_sizes(blocks)[0], D), F32) for blocks in ROUND_BLOCKS]
+        + [pltpu.VMEM((6, sum(round_sizes(blocks)[2]), D), F32) for blocks in ROUND_BLOCKS]
         + [dma((10,)), dma((4,)), dma((4,)), dma((4,))]
-        + [dma((4, 6)), dma((4, 6)), dma((4, 6, 6)), dma((4, 6, 6)), dma((4, 3, 6)), dma((4, 3, 6)), dma((4, 4, 6)),
-           dma((4, 4, 6)), regular((4, 3, 6)), regular((4, 6)), dma((7,)), dma((7,))],
+        + [dma((5,)), dma((5,)), dma((5,)), dma((5, 6)), dma((5,)), dma((5, 3)), dma((5,)), dma((5,)), regular((5, 3)),
+           regular((5,)), dma((1,)), dma((7,))],
         compiler_params=pltpu.CompilerParams(collective_id=0, has_side_effects=True, vmem_limit_bytes=STEP_VMEM),
         cost_estimate=pl.CostEstimate(flops=12_000_000_000, bytes_accessed=30_000_000, transcendentals=0),
     )(latents.reshape(T, D), cotangent.reshape(T, D), ln_params, w_qkv, w_out.reshape(2, D, D), w_up, w_down)

time: 164 us -> 155 us (0.945)
  Pallas kernels: 163 us -> 154 us
    pallas_call x1, Pallas kernels: 157 us -> 148 us  [device_step(): pl.pallas_call(functools.partial(step_kernel, n), out_shape=[pltpu.VMEM(s...]
where the time goes in v4:
time: 155 us
  Pallas kernels  154 us (99%)
    pallas_call x1, Pallas kernels, device_step(): pl.pallas_call(functools.partial(step_kernel, n), out_shape=[pltpu.VMEM(s...  148 us
    pallas_call x1, Pallas kernels, device_step(): pl.pallas_call(publish_kernel, out_shape=[jax.ShapeDtypeStruct(s, t) for...  5.5 us

profile of v4, /device:TPU:1, one launch (start us, length us, event | category | flops | bytes accessed | tf_op | source)
XLA Modules:
  0.0 154.6 jit_solution(9880356093135436403)
XLA Ops:
  0.6 148.3 %shard_map.126 = (bf16[512,384]{1,0:T(8,128)(2,1)S(1)}, bf16[512,384]{1,0:T(8,128)(2,1)S(1)}, f32[2,4,384]{2,1,0:T(4,128)S(1)}, f32[2,12,384,384]{3,2,1,0:T(8,128)S(1)}) custom-call(bf16[512,384]{1,0:T(8,128)(2,1)} %bitcast.8, bf16[512,384]{1,0:T(8,128)(2,1)} %bitcast.9, bf16[2,4,384]{2,1,0:T(4,128)(2,1)} %ln_in.1, bf16[2,384,1152]{2,1,0:T(8,128)(2,1)} %wqkv_hbm.1, ...), custom_call_target="tpu_custom_call" | custom-call | flops 12000000000 | bytes 30000000 | tf_op jit(solution)/shard_map/pallas_call | solution.py:588
  148.9 5.5 %shard_map.127 = (bf16[512,384]{1,0:T(8,128)(2,1)}, bf16[512,384]{1,0:T(8,128)(2,1)}, f32[2,4,384]{2,1,0:T(4,128)}, f32[2,384,1152]{2,1,0:T(8,128)}, f32[2,384,3...) custom-call(bf16[512,384]{1,0:T(8,128)(2,1)S(1)} %get-tuple-element.18.y_in, ...), custom_call_target="tpu_custom_call" | custom-call | tf_op jit(solution)/shard_map/pallas_call | solution.py:607

commit v5 on v4

v5 whole, which is shorter than its diff:
```python
import functools

import jax
import jax.numpy as jnp
from jax import lax
from jax.experimental import pallas as pl
from jax.experimental.pallas import tpu as pltpu
from jax.sharding import PartitionSpec as P

F32 = jnp.float32
BF16 = jnp.bfloat16
D = 384
T = 512
SEQ = 256
FF = 1536
WIDTH = 256
MESH = pl.DeviceIdType.MESH
STEP_VMEM = 51_500_000
GELU_C = 0.7978845608028654
GELU_A = 0.044715


def dot_nn(a, b):
    return lax.dot_general(a, b, (((1,), (0,)), ((), ())), preferred_element_type=F32)


def dot_nt(a, b):
    return lax.dot_general(a, b, (((1,), (1,)), ((), ())), preferred_element_type=F32)


def dot_tn(a, b):
    return lax.dot_general(a, b, (((0,), (0,)), ((), ())), preferred_element_type=F32)


def ln_norm(x32):
    mean = jnp.sum(x32, axis=-1, keepdims=True) * (1.0 / D)
    centered = x32 - mean
    inv_std = lax.rsqrt(jnp.sum(centered * centered, axis=-1, keepdims=True) * (1.0 / D) + 1e-6)
    return centered * inv_std, inv_std


def ln_back(d32, normed, inv_std, gain):
    d_norm = d32 * gain
    d_center = d_norm - jnp.sum(d_norm, axis=-1, keepdims=True) * (1.0 / D)
    return inv_std * (d_center - normed * (jnp.sum(d_norm * normed, axis=-1, keepdims=True) * (1.0 / D)))


def seq_loop(body, between=None):
    def step(seq, _):
        body(seq, pl.ds(pl.multiple_of(seq * SEQ, SEQ), SEQ))
        if between is not None:
            pl.when(seq == 0)(between)
        return 0
    lax.fori_loop(0, 2, step, 0)


HEAD_CUTS = (slice(0, 64), slice(64, 128))
SCORE_EXP2 = 0.125 * 1.4426950408889634


def pair_cols(which, pair):
    return slice(which * D + pair * 128, which * D + (pair + 1) * 128)


def attn_forward(x_ref, ln_ref, wqkv_ref, qkv_s, p_s, o_s):
    normed, _ = ln_norm(x_ref[...].astype(F32))
    a_in = (normed * ln_ref[0:1, :] + ln_ref[1:2, :]).astype(BF16)
    qkv_s[...] = dot_nn(a_in, wqkv_ref[...]).astype(BF16)

    def heads(seq, rows):
        for pair in range(3):
            q2, k2, v2 = (qkv_s[rows, pair_cols(which, pair)] for which in range(3))
            scores = [dot_nt(q2[:, cut], k2[:, cut]) for cut in HEAD_CUTS]
            outs = []
            for e in range(2):
                top = jnp.max(scores[e], axis=-1, keepdims=True)
                expd = jnp.exp2((scores[e] - top) * SCORE_EXP2)
                total = jnp.sum(expd, axis=-1, keepdims=True)
                probs = (expd * (1.0 / total)).astype(BF16)
                p_s[seq * 6 + pair * 2 + e] = probs
                outs.append(probs)
            o_s[rows, pair_cols(0, pair)] = jnp.concatenate(
                [dot_nn(outs[e], v2[:, HEAD_CUTS[e]]).astype(BF16) for e in range(2)], axis=1)
    seq_loop(heads)


def hidden(x_ref, o_s, wout_ref):
    hid = (x_ref[...].astype(F32) + dot_nn(o_s[...], wout_ref[...])).astype(BF16)
    return hid


def gelu_parts(up):
    up2 = up * up
    tanh = jnp.tanh(GELU_C * up * (1.0 + GELU_A * up2))
    half = 0.5 + 0.5 * tanh
    return up2, tanh, half


def ff_cols():
    return [slice(c, c + WIDTH) for c in range(0, FF, WIDTH)]


def gelu_slope(up, up2, tanh, half):
    return half + (0.5 * up) * (1.0 - tanh * tanh) * (GELU_C + (3.0 * GELU_A * GELU_C) * up2)


def mlp_input(hid32, ln_ref):
    normed, inv_std = ln_norm(hid32)
    return (normed * ln_ref[2:3, :] + ln_ref[3:4, :]).astype(BF16), normed, inv_std


def mlp_forward(hid32, ln_ref, wup_ref, wdown_ref, act_s):
    m_in, _, _ = mlp_input(hid32, ln_ref)
    for cols in ff_cols():
        up = dot_nn(m_in, wup_ref[:, cols])
        act_s[:, cols] = (up * gelu_parts(up)[2]).astype(BF16)
    return (hid32 + dot_nn(act_s[...], wdown_ref[...])).astype(BF16)


def hidden_backward(dm, normed, inv_std, dy, ln_ref, wout_ref, dhid_s, datt_s, lng_ref, rows):
    dm32 = dm.astype(BF16).astype(F32)
    lng_ref[2:3, :] += jnp.sum(dm32 * normed, axis=0, keepdims=True)
    lng_ref[3:4, :] += jnp.sum(dm32, axis=0, keepdims=True)
    d_hid32 = ln_back(dm32, normed, inv_std, ln_ref[2:3, :])
    d_hid = (d_hid32 + dy.astype(F32)).astype(BF16)
    dhid_s[rows, :] = d_hid
    datt_s[rows, :] = dot_nt(d_hid, wout_ref[...]).astype(BF16)


def mlp_both_ways(hid32, dy_ref, ln_ref, wup_ref, wout_ref, wdown_ref, m_s, act_s, dup_s, dhid_s, datt_s, lng_ref, out_ref):
    m_in, normed, inv_std = mlp_input(hid32, ln_ref)
    m_s[...] = m_in
    dy = dy_ref[...]
    total = None
    dm = None
    for cols in ff_cols():
        up = dot_nn(m_in, wup_ref[:, cols])
        up2, tanh, half = gelu_parts(up)
        act = (up * half).astype(BF16)
        act_s[:, cols] = act
        part = dot_nn(act, wdown_ref[cols, :])
        total = part if total is None else total + part
        d_act = dot_nt(dy, wdown_ref[cols, :]).astype(BF16).astype(F32)
        d_up = (d_act * gelu_slope(up, up2, tanh, half)).astype(BF16)
        dup_s[:, cols] = d_up
        d_part = dot_nt(d_up, wup_ref[:, cols])
        dm = d_part if dm is None else dm + d_part
    out_ref[...] = (hid32 + total).astype(BF16)
    hidden_backward(dm, normed, inv_std, dy, ln_ref, wout_ref, dhid_s, datt_s, lng_ref, pl.ds(0, T))


def mlp_prepare(h_s, ln_ref, wup_ref, m_s, act_s, slope_ref):
    def tile(i, rows):
        m_in, _, _ = mlp_input(h_s[rows, :].astype(F32), ln_ref)
        m_s[rows, :] = m_in
        for c, cols in enumerate(ff_cols()):
            up = dot_nn(m_in, wup_ref[:, cols])
            up2, tanh, half = gelu_parts(up)
            act_s[rows, cols] = (up * half).astype(BF16)
            slope_ref[i * 6 + c, 0:SEQ, 0:WIDTH] = gelu_slope(up, up2, tanh, half)
    seq_loop(tile)


def mlp_backward(h_s, dy_ref, slope_ref, ln_ref, wup_ref, wout_ref, wdown_ref, dup_s, dhid_s, datt_s, lng_ref, between):
    def tile(i, rows):
        dy = dy_ref[rows, :]
        for c, cols in enumerate(ff_cols()):
            d_act = dot_nt(dy, wdown_ref[cols, :]).astype(BF16).astype(F32)
            dup_s[rows, cols] = (d_act * slope_ref[i * 6 + c, 0:SEQ, 0:WIDTH]).astype(BF16)
        normed, inv_std = ln_norm(h_s[rows, :].astype(F32))
        hidden_backward(dot_nt(dup_s[rows, :], wup_ref[...]), normed, inv_std, dy, ln_ref, wout_ref, dhid_s, datt_s, lng_ref,
                        rows)
    seq_loop(tile, between)


def mlp_grads_first(g_ref, m_s, act_s, dup_s, dy_ref):
    up = dot_tn(m_s[...], dup_s[...])
    for c in range(4):
        g_ref[4 + c] = up[:, c * D:(c + 1) * D]
    down = dot_tn(act_s[:, 0:2 * D], dy_ref[...])
    for c in range(2):
        g_ref[8 + c] = down[c * D:(c + 1) * D, :]


def mlp_grads_last(g_ref, act_s, dhid_s, o_s, dy_ref):
    down = dot_tn(act_s[:, 2 * D:4 * D], dy_ref[...])
    for c in range(2):
        g_ref[10 + c] = down[c * D:(c + 1) * D, :]
    g_ref[3] = dot_tn(o_s[...], dhid_s[...])


def attn_backward(qkv_s, p_s, datt_s, dqkv_s, between):
    def heads(seq, rows):
        for pair in range(3):
            q2, k2, v2 = (qkv_s[rows, pair_cols(which, pair)] for which in range(3))
            do2 = datt_s[rows, pair_cols(0, pair)]
            base = seq * 6 + pair * 2
            d_probs = [dot_nt(do2[:, cut], v2[:, cut]) for cut in HEAD_CUTS]
            d_value = [dot_tn(p_s[base + e], do2[:, HEAD_CUTS[e]]).astype(BF16) for e in range(2)]
            d_scores = []
            for e in range(2):
                d32 = d_probs[e].astype(BF16).astype(F32)
                p32 = p_s[base + e].astype(F32)
                row_dot = jnp.sum(d32 * p32, axis=-1, keepdims=True)
                d_scores.append((p32 * (d32 - row_dot) * 0.125).astype(BF16))
            d_query = [dot_nn(d_scores[e], k2[:, HEAD_CUTS[e]]).astype(BF16) for e in range(2)]
            d_key = [dot_tn(d_scores[e], q2[:, HEAD_CUTS[e]]).astype(BF16) for e in range(2)]
            for which, parts in enumerate((d_query, d_key, d_value)):
                dqkv_s[rows, pair_cols(which, pair)] = jnp.concatenate(parts, axis=1)
    seq_loop(heads, between)


def qkv_backward(x_ref, dqkv_s, dhid_s, ln_ref, wqkv_ref, a_s, dx_ref, lng_ref):
    normed, inv_std = ln_norm(x_ref[...].astype(F32))
    a_s[...] = (normed * ln_ref[0:1, :] + ln_ref[1:2, :]).astype(BF16)
    da32 = dot_nt(dqkv_s[...], wqkv_ref[...]).astype(BF16).astype(F32)
    lng_ref[0:1, :] += jnp.sum(da32 * normed, axis=0, keepdims=True)
    lng_ref[1:2, :] += jnp.sum(da32, axis=0, keepdims=True)
    d_in = ln_back(da32, normed, inv_std, ln_ref[0:1, :])
    dx_ref[...] = (d_in + dhid_s[...].astype(F32)).astype(BF16)


def qkv_grads(g_ref, a_s, dqkv_s):
    out = dot_tn(a_s[...], dqkv_s[...])
    for c in range(3):
        g_ref[c] = out[:, c * D:(c + 1) * D]


def to_pieces(act_s, snd_ref):
    for a in range(2):
        snd_ref[:, a] = act_s[a * SEQ:(a + 1) * SEQ, :].reshape(SEQ // 2, 2, D)


def from_pieces(rcv_ref, dst_ref):
    flat = rcv_ref[...].reshape(T, D)
    row = lax.broadcasted_iota(jnp.int32, (SEQ, T), 0)
    col = lax.broadcasted_iota(jnp.int32, (SEQ, T), 1)
    for b in range(2):
        pick = (col == 2 * row + b).astype(F32).astype(BF16)
        dst_ref[b * SEQ:(b + 1) * SEQ, :] = dot_nn(pick, flat).astype(BF16)


EXCHANGE = 24
ROUND_BLOCKS = ((4, 5, 6, 7, 8, 9), (10, 11, 3, 0, 1, 2), (4, 5, 6, 7, 8, 9), (10, 11, 3, 0, 1, 2))
ROUND_SIDE = (1, 1, 0, 0)
ROUNDS = len(ROUND_SIDE)
SCHEDULE = {
    "b": "",
    "c0": "",
    "c1": "1",
    "e": "",
    "f": "12",
    "h0": "",
    "h1": "",
    "i": "1",
    "j": "",
    "k0": "2",
    "k1": "13",
    "l": "",
    "tail": "2514321543215432145321435214352435243434",
}


def round_sizes(blocks):
    keep = rows = D * len(blocks) // 12
    sizes = []
    while rows > EXCHANGE:
        rows //= 2
        sizes.append(rows)
    return keep, len(sizes), sizes + [EXCHANGE] * (6 - len(sizes))


def dim_info(me, dim):
    axis, far = dim // 2, dim % 2
    stride = (2, 8, 32)[axis]
    coord = lax.rem(lax.div(me, stride), 4)
    if far:
        bit = lax.div(coord, 2)
        partner = me + (3 - 2 * coord) * stride
    else:
        bit = lax.rem(coord + lax.div(coord, 2), 2)
        partner = me + (1 - 2 * lax.rem(coord, 2)) * stride
    return bit, partner


def remote_copy(src, dst, s_sem, r_sem, to):
    return pltpu.make_async_remote_copy(src, dst, s_sem, r_sem, device_id={"sp": to}, device_id_type=MESH)


def rows_at(start, size):
    return pl.ds(pl.multiple_of(start, 8), size)


class Round:
    def __init__(self, index, grads, me, dims, half, recv, sems):
        self.r = index
        self.g = grads.at[ROUND_SIDE[index]]
        self.keep, self.halvings, self.sizes = round_sizes(ROUND_BLOCKS[index])
        self.dims = dims
        self.half = half
        self.recv = recv
        core = lax.rem(me, 2)
        self.sibling = me + 1 - 2 * core
        (self.half_send, self.half_recv, self.send_sem, self.recv_sem, self.back_send, self.back_recv,
         self.fwd_send, self.fwd_recv, self.free_sem, self.core_free) = sems
        per_block = 6 // len(ROUND_BLOCKS[index])
        self.block = [ROUND_BLOCKS[index][p // per_block] for p in range(6)]
        first = [2 * self.keep * (p % per_block) for p in range(6)]
        self.away = [first[p] + (1 - core) * self.keep for p in range(6)]
        self.offs = {(p, 0): first[p] + core * self.keep for p in range(6)}
        self.give = {}
        for p in range(6):
            for t in range(6):
                off, size, bit = self.offs[p, t], self.sizes[t], dims[(p + t) % 6][0]
                halve = t < self.halvings
                self.offs[p, t + 1] = off + bit * size if halve else off
                self.give[p, t] = off + (1 - bit) * size if halve else off

    def rows(self, p, off, size):
        return self.g.at[self.block[p], rows_at(off, size)]

    def partner(self, t, p):
        return self.dims[(p + t) % 6][1]

    def core_copy(self, p):
        return remote_copy(self.rows(p, self.away[p], self.keep), self.half.at[p], self.half_send.at[self.r],
                           self.half_recv.at[self.r], self.sibling)

    def recv_rows(self, t):
        return pl.ds(sum(self.sizes[:t]), self.sizes[t])

    def send_copy(self, t, p):
        return remote_copy(self.rows(p, self.give[p, t], self.sizes[t]), self.recv.at[p, self.recv_rows(t)],
                           self.send_sem.at[self.r], self.recv_sem.at[self.r, t], self.partner(t, p))

    def back_copy(self, t, p):
        rows = self.rows(p, self.offs[p, t + 1], self.sizes[t])
        return remote_copy(rows, rows, self.back_send.at[self.r], self.back_recv.at[self.r, t], self.partner(t, p))

    def forward_copy(self, slot, p):
        last = self.halvings
        if slot == 0:
            rows = self.rows(p, self.offs[p, last], self.sizes[last - 1])
        else:
            rows = self.rows(p, self.give[p, last - slot], self.sizes[last - slot])
        return remote_copy(rows, rows, self.fwd_send.at[self.r], self.fwd_recv.at[self.r], self.sibling)

    def wait_bytes(self, ref, *semaphores):
        for sem in semaphores:
            pltpu.make_async_copy(ref, ref, sem).wait()

    def start_core(self):
        for p in range(6):
            self.core_copy(p).start()

    def join_core(self):
        self.wait_bytes(self.half, self.half_send.at[self.r], self.half_recv.at[self.r])
        pl.semaphore_signal(self.core_free.at[self.r], inc=1, device_id={"sp": self.sibling}, device_id_type=MESH)
        for p in range(6):
            self.g[self.block[p], rows_at(self.offs[p, 0], self.keep)] += self.half[p]
            self.send_copy(0, p).start()

    def start_back(self, t):
        pl.semaphore_wait(self.free_sem.at[self.r, t], 6)
        for p in range(6):
            self.back_copy(t, p).start()

    def step(self, t):
        size = self.sizes[t]
        self.wait_bytes(self.recv.at[:, self.recv_rows(t)], self.send_sem.at[self.r], self.recv_sem.at[self.r, t])
        for p in range(6):
            if t < self.halvings:
                pl.semaphore_signal(self.free_sem.at[self.r, t], inc=1, device_id={"sp": self.partner(t, p)},
                                    device_id_type=MESH)
            self.g[self.block[p], rows_at(self.offs[p, t + 1], size)] += self.recv[p, self.recv_rows(t)]
            if t < 5:
                self.send_copy(t + 1, p).start()
        if t == 5:
            self.start_back(self.halvings - 1)
            pl.semaphore_wait(self.core_free.at[self.r], 1)
            for p in range(6):
                self.forward_copy(0, p).start()

    def back(self, t):
        self.wait_bytes(self.recv.at[:, self.recv_rows(t)], self.back_send.at[self.r], self.back_recv.at[self.r, t])
        if t > 0:
            self.start_back(t - 1)
        for p in range(6):
            self.forward_copy(self.halvings - t, p).start()

    def steps(self):
        yield self.join_core()
        for t in range(6):
            yield self.step(t)
        for t in reversed(range(self.halvings)):
            yield self.back(t)

    def finish(self):
        self.wait_bytes(self.half, self.fwd_send.at[self.r], self.fwd_recv.at[self.r])


def out_slices(blk, gqkv, gout, gup, gdown):
    cols = [pl.ds(c * D, D) for c in range(4)]
    return ([gqkv.at[blk, :, cols[c]] for c in range(3)] + [gout.at[blk]] + [gup.at[blk, :, cols[c]] for c in range(4)]
            + [gdown.at[blk, cols[c]] for c in range(4)])


def step_kernel(n, x_hbm, cot_hbm, ln_in, wqkv_hbm, wout_hbm, wup_hbm, wdown_hbm,
                y_ref, dx_ref, gln_ref, grads,
                x_s, cot_s, mid_s, dmid_s, h_s, ln_s, wqkv, wout, wup, wdown, qkv_s, p_s, o_s,
                m_s, act_s, dup_s, dhid_s, datt_s, dqkv_s, a_s, m0_s, act0_s, snd, rcv, lnacc, lnrecv, *rest):
    halves, recvs = rest[:ROUNDS], rest[ROUNDS:2 * ROUNDS]
    (load_sem, swap_send, swap_recv, swap_local, *sems) = rest[2 * ROUNDS:]
    me = lax.axis_index("sp")
    dims = [dim_info(me, d) for d in range(6)]
    sibling = me + 1 - 2 * lax.rem(me, 2)
    ln_send, ln_recv = sems[-2:]
    sems = sems[:-2]

    loads = {}
    for name, src, dst in (("x", x_hbm, x_s), ("qkv0", wqkv_hbm.at[0], wqkv.at[0]), ("cot", cot_hbm, cot_s),
                           ("out0", wout_hbm.at[0], wout.at[0]), ("up0", wup_hbm.at[0], wup.at[0]),
                           ("down0", wdown_hbm.at[0], wdown.at[0]), ("qkv1", wqkv_hbm.at[1], wqkv.at[1]),
                           ("out1", wout_hbm.at[1], wout.at[1]), ("up1", wup_hbm.at[1], wup.at[1]),
                           ("down1", wdown_hbm.at[1], wdown.at[1])):
        loads[name] = pltpu.make_async_copy(src, dst, load_sem.at[len(loads)])
        loads[name].start()

    barrier = pltpu.get_barrier_semaphore()

    def greet_one(k):
        pl.semaphore_signal(barrier, inc=1, device_id={"sp": lax.rem(me + k, n)}, device_id_type=MESH)

    def greet(k, _):
        for j in range(4):
            greet_one(4 * k + 1 + j)
        return 0
    lax.fori_loop(0, (n - 1) // 4, greet, 0)
    for k in range((n - 1) // 4 * 4 + 1, n):
        greet_one(k)

    def need(*names):
        for name in names:
            loads[name].wait()

    def remote_piece(i, k):
        to = lax.rem(me + k, n)
        return remote_copy(snd.at[i % 2, to], rcv.at[i, me], swap_send.at[i], swap_recv.at[i], to)

    def start_swap(i):
        pltpu.make_async_copy(snd.at[i % 2, me], rcv.at[i, me], swap_local.at[i]).start()

        def send(k, _):
            for j in range(4):
                remote_piece(i, 4 * k + 1 + j).start()
            return 0
        lax.fori_loop(0, (n - 1) // 4, send, 0)
        for k in range((n - 1) // 4 * 4 + 1, n):
            remote_piece(i, k).start()

    def end_swap(i):
        pltpu.make_async_copy(snd.at[i % 2, me], rcv.at[i, me], swap_local.at[i]).wait()
        rest = pl.ds(0, n - 1)
        pltpu.make_async_copy(snd.at[i % 2, rest], rcv.at[i, rest], swap_send.at[i]).wait()
        pltpu.make_async_copy(snd.at[i % 2, rest], rcv.at[i, rest], swap_recv.at[i]).wait()

    ln_s[...] = ln_in[...].astype(F32)
    lnacc[...] = jnp.zeros_like(lnacc)
    ln = [ln_s.at[i] for i in range(2)]
    lng = [lnacc.at[pl.ds(8 * i, 8)] for i in range(2)]
    saved = [(qkv_s.at[i], p_s.at[i], o_s.at[i]) for i in range(2)]
    rounds = [Round(r, grads, me, dims, halves[r], recvs[r], sems) for r in range(ROUNDS)]
    r1, r2, r3, r4 = rounds

    def ln_copy(t):
        to = sibling if t == 0 else dims[t - 1][1]
        return remote_copy(lnacc, lnrecv.at[t], ln_send.at[0], ln_recv.at[t], to)

    def ln_next(t):
        ln_copy(t).wait()
        lnacc[...] += lnrecv[t]
        if t < 6:
            ln_copy(t + 1).start()

    def ln_steps():
        for t in range(7):
            yield ln_next(t)

    walks = [rnd.steps() for rnd in rounds] + [ln_steps()]

    def slot(name):
        for digit in SCHEDULE[name]:
            next(walks[int(digit) - 1])

    need("x", "qkv0")
    attn_forward(x_s, ln[0], wqkv.at[0], *saved[0])
    need("cot")
    to_pieces(cot_s, snd.at[0])
    need("out0", "up0", "down0")
    h_s[...] = hidden(x_s, o_s.at[0], wout.at[0])
    mid_s[...] = mlp_forward(h_s[...].astype(F32), ln[0], wup.at[0], wdown.at[0], act0_s)
    to_pieces(mid_s, snd.at[1])
    pl.semaphore_wait(barrier, n - 1)
    start_swap(1)
    start_swap(0)
    slopes = grads.at[0]
    mlp_prepare(h_s, ln[0], wup.at[0], m0_s, act0_s, slopes)

    need("qkv1", "out1", "up1", "down1")
    end_swap(1)
    from_pieces(rcv.at[1], mid_s)
    attn_forward(mid_s, ln[1], wqkv.at[1], *saved[1])
    end_swap(0)
    from_pieces(rcv.at[0], cot_s)
    mlp_both_ways(hidden(mid_s, o_s.at[1], wout.at[1]).astype(F32), cot_s, ln[1], wup.at[1], wout.at[1], wdown.at[1], m_s, act_s,
                  dup_s, dhid_s, datt_s, lng[1], y_ref)
    to_pieces(y_ref, snd.at[0])
    start_swap(2)
    mlp_grads_first(grads.at[1], m_s, act_s, dup_s, cot_s)
    r1.start_core()
    slot("b")
    attn_backward(qkv_s.at[1], p_s.at[1], datt_s, dqkv_s, lambda: slot("c0"))
    slot("c1")
    qkv_backward(mid_s, dqkv_s, dhid_s, ln[1], wqkv.at[1], a_s, dmid_s, lng[1])
    to_pieces(dmid_s, snd.at[1])
    start_swap(3)
    mlp_grads_last(grads.at[1], act_s, dhid_s, o_s.at[1], cot_s)
    qkv_grads(grads.at[1], a_s, dqkv_s)
    r2.start_core()
    slot("e")
    end_swap(2)
    from_pieces(rcv.at[2], y_ref)
    slot("f")
    end_swap(3)
    from_pieces(rcv.at[3], dmid_s)

    mlp_backward(h_s, dmid_s, slopes, ln[0], wup.at[0], wout.at[0], wdown.at[0], dup_s, dhid_s, datt_s, lng[0],
                 lambda: slot("h0"))
    slot("h1")
    mlp_grads_first(grads.at[0], m0_s, act0_s, dup_s, dmid_s)
    r3.start_core()
    slot("i")
    mlp_grads_last(grads.at[0], act0_s, dhid_s, o_s.at[0], dmid_s)
    slot("j")
    attn_backward(qkv_s.at[0], p_s.at[0], datt_s, dqkv_s, lambda: slot("k0"))
    slot("k1")
    qkv_backward(x_s, dqkv_s, dhid_s, ln[0], wqkv.at[0], a_s, dx_ref, lng[0])
    ln_copy(0).start()
    slot("l")
    qkv_grads(grads.at[0], a_s, dqkv_s)
    r4.start_core()
    slot("tail")
    for rnd in rounds:
        rnd.finish()
    for i in range(2):
        gln_ref[i] = lnacc[8 * i:8 * i + 4, :]


def publish_kernel(y_in, dx_in, gln_in, grads, y_ref, dx_ref, gln_ref, gqkv, gout, gup, gdown, sem):
    pairs = [(y_in, y_ref), (dx_in, dx_ref), (gln_in, gln_ref)]
    for i in range(2):
        slices = out_slices(i, gqkv, gout, gup, gdown)
        pairs += [(grads.at[i, j], slices[j]) for j in range(12)]
    copies = [pltpu.make_async_copy(src, dst, sem.at[k]) for k, (src, dst) in enumerate(pairs)]
    for copy in copies:
        copy.start()
    for copy in copies:
        copy.wait()


def device_step(n, latents, cotangent, ln_params, w_qkv, w_out, w_up, w_down):
    dma = pltpu.SemaphoreType.DMA
    regular = pltpu.SemaphoreType.REGULAR
    any_spec = pl.BlockSpec(memory_space=pl.ANY)
    vmem_spec = pl.BlockSpec(memory_space=pltpu.VMEM)
    act, wide, qkv = (T, D), (T, FF), (T, 3 * D)
    shapes = [(act, BF16), (act, BF16), ((2, 4, D), F32)]
    held = pl.pallas_call(
        functools.partial(step_kernel, n),
        out_shape=[pltpu.VMEM(s, t) for s, t in shapes] + [pltpu.VMEM((2, 12, D, D), F32)],
        in_specs=[any_spec, any_spec, vmem_spec] + [any_spec] * 4,
        out_specs=[vmem_spec] * 4,
        scratch_shapes=[pltpu.VMEM(s, BF16) for s in [act] * 5]
        + [pltpu.VMEM((2, 4, D), F32)]
        + [pltpu.VMEM((2,) + s, BF16) for s in ((D, 3 * D), (D, D), (D, FF), (FF, D), qkv, (12, SEQ, SEQ), act)]
        + [pltpu.VMEM(s, BF16) for s in (act, wide, wide, act, act, qkv, act, act, wide)]
        + [pltpu.VMEM((2, n, 2, 2, D), BF16), pltpu.VMEM((4, n, 2, 2, D), BF16)]
        + [pltpu.VMEM((16, D), F32), pltpu.VMEM((7, 16, D), F32)]
        + [pltpu.VMEM((6, round_sizes(blocks)[0], D), F32) for blocks in ROUND_BLOCKS]
        + [pltpu.VMEM((6, sum(round_sizes(blocks)[2]), D), F32) for blocks in ROUND_BLOCKS]
        + [dma((10,)), dma((4,)), dma((4,)), dma((4,))]
        + [dma((ROUNDS,))] * 3 + [dma((ROUNDS, 6)), dma((ROUNDS,)), dma((ROUNDS, 3)), dma((ROUNDS,)), dma((ROUNDS,))]
        + [regular((ROUNDS, 3)), regular((ROUNDS,)), dma((1,)), dma((7,))],
        compiler_params=pltpu.CompilerParams(collective_id=0, has_side_effects=True, vmem_limit_bytes=STEP_VMEM),
        cost_estimate=pl.CostEstimate(flops=12_000_000_000, bytes_accessed=30_000_000, transcendentals=0),
    )(latents.reshape(T, D), cotangent.reshape(T, D), ln_params, w_qkv, w_out.reshape(2, D, D), w_up, w_down)
    y, dx, gln, gqkv, gout, gup, gdown = pl.pallas_call(
        publish_kernel,
        out_shape=[jax.ShapeDtypeStruct(s, t) for s, t in shapes]
        + [jax.ShapeDtypeStruct(s, F32) for s in ((2, D, 3 * D), (2, D, D), (2, D, FF), (2, FF, D))],
        in_specs=[vmem_spec] * 4,
        out_specs=[any_spec] * 7,
        scratch_shapes=[dma((27,))],
        compiler_params=pltpu.CompilerParams(vmem_limit_bytes=2_000_000),
    )(*held)
    return (y.reshape(latents.shape), dx.reshape(latents.shape), gln, gqkv, gout.reshape(2, 6, 64, D), gup, gdown)


def solution(mesh):
    act_spec = P('data', 'sp', None, None)
    replicated = P()
    part_spec = P('data')
    return jax.shard_map(functools.partial(device_step, mesh.shape["sp"]), mesh=mesh,
                         in_specs=(act_spec, act_spec, replicated, replicated, replicated, replicated, replicated),
                         out_specs=(act_spec, act_spec, part_spec, part_spec, part_spec, part_spec, part_spec),
                         check_vma=False)
```

time: 155 us -> 124 us (0.80)
  Pallas kernels: 154 us -> 123 us
    pallas_call x1, Pallas kernels: 148 us -> 117 us  [device_step(): pl.pallas_call(functools.partial(step_kernel, n), out_shape=[pltpu.VMEM(s...]
where the time goes in v5:
time: 124 us
  Pallas kernels  123 us (99%)
    pallas_call x1, Pallas kernels, device_step(): pl.pallas_call(functools.partial(step_kernel, n), out_shape=[pltpu.VMEM(s...  117 us
    pallas_call x1, Pallas kernels, device_step(): pl.pallas_call(publish_kernel, out_shape=[jax.ShapeDtypeStruct(s, t) for...  5.5 us

profile of v5, /device:TPU:1, one launch (start us, length us, event | category | flops | bytes accessed | tf_op | source)
XLA Modules:
  0.0 123.6 jit_solution(10734816360108144142)
XLA Ops:
  0.6 117.3 %shard_map.126 = (bf16[512,384]{1,0:T(8,128)(2,1)S(1)}, bf16[512,384]{1,0:T(8,128)(2,1)S(1)}, f32[2,4,384]{2,1,0:T(4,128)S(1)}, f32[2,12,384,384]{3,2,1,0:T(8,128)S(1)}) custom-call(bf16[512,384]{1,0:T(8,128)(2,1)} %bitcast.8, bf16[512,384]{1,0:T(8,128)(2,1)} %bitcast.9, bf16[2,4,384]{2,1,0:T(4,128)(2,1)} %ln_in.1, bf16[2,384,1152]{2,1,0:T(8,128)(2,1)} %wqkv_hbm.1, ...), custom_call_target="tpu_custom_call" | custom-call | flops 12000000000 | bytes 30000000 | tf_op jit(solution)/shard_map/pallas_call | solution.py:578
  117.9 5.5 %shard_map.127 = (bf16[512,384]{1,0:T(8,128)(2,1)}, bf16[512,384]{1,0:T(8,128)(2,1)}, f32[2,4,384]{2,1,0:T(4,128)}, f32[2,384,1152]{2,1,0:T(8,128)}, f32[2,384,3...) custom-call(bf16[512,384]{1,0:T(8,128)(2,1)S(1)} %get-tuple-element.18.y_in, ...), custom_call_target="tpu_custom_call" | custom-call | tf_op jit(solution)/shard_map/pallas_call | solution.py:597
